TPU v7x, 32 devices: a whole 2x2x4 slice. The times are simulated.
32 devices in a mesh: rep: 2 (over x), shard: 16 (over z, y, core).
Axes of the slice: x: 2, y: 2, z: 4, core: 2. Of those that a mesh axis runs over, the one named last changes fastest.
Arguments:
- tokens_x: bfloat16 [8192, 4096], P(('rep', 'shard')), may hold values from -6 to 6
- key_grad: bfloat16 [8192, 1024], P(('rep', 'shard')), may hold values from -0.06591797 to 0.06591797
- left_root: bfloat16 [64, 512, 512], P('shard'), may hold values from -1 to 3
- slot_grads: bfloat16 [64, 512, 512], P('shard'), may hold values from -6 to 6
- right_root: bfloat16 [64, 512, 512], P('shard'), may hold values from -1 to 3
- block_slot: int32 [32], replicated, may hold values from 0 to 63, as said below
Outputs:
- grad_key: float32 [4096, 1024], P('shard')
- update: bfloat16 [512, 32, 512], P('shard')
Inputs may be any that keep to these rules, and one draw needn't show every extreme that they name: `block_slot`: the entries are distinct; slot v is slot v % 4 of shard index v // 4; no shard index holds more than 4 blocks, and some shard index holds exactly 4.
All inputs are finite; a program needn't handle non-finite values.
Results may differ from a plain program's by a relative error of at most 0.006.
Values may be sent and summed in bfloat16 or wider, within the bound.
No kernel may reach another device: no remote copies, remote signals or barrier semaphores. Data moves between devices by JAX's collectives and lax.ppermute only.
A program may use at most 128 MiB of HBM per device.

v0:
```python
import jax
import jax.numpy as jnp
from jax import lax
from jax.sharding import PartitionSpec as P


def column_term(features, cotangent):
    return lax.dot_general(
        features, cotangent, (((0,), (0,)), ((), ())), preferred_element_type=jnp.float32
    )


def precondition(left_block, grad_block, right_block):
    left_part = jnp.einsum(
        "sij,sjk->sik", left_block, grad_block, preferred_element_type=jnp.float32
    ).astype(jnp.bfloat16)
    return jnp.einsum(
        "sij,sjk->isk", left_part, right_block, preferred_element_type=jnp.float32
    ).astype(jnp.bfloat16)


def shards(tokens_x, key_grad, left_root, slot_grads, right_root, block_slot):
    n_shard = lax.axis_size("shard")
    n_rep = lax.axis_size("rep")
    own_rows = lax.psum_scatter(
        column_term(tokens_x, key_grad), "shard", scatter_dimension=0, tiled=True
    )
    grad_key = lax.psum(own_rows, "rep")
    slot_count = left_root.shape[0]
    half_slots = slot_count // n_rep
    first_slot = lax.axis_index("rep") * half_slots

    def own_half(values):
        return lax.dynamic_slice_in_dim(values, first_slot, half_slots, 0)

    product = precondition(own_half(left_root), own_half(slot_grads), own_half(right_root))
    received = lax.all_to_all(product, "shard", split_axis=0, concat_axis=1, tiled=True)
    joined = lax.all_gather(received, "rep", axis=1, tiled=True)
    owner = block_slot // slot_count
    within = block_slot % slot_count
    position = (
        within // half_slots * (n_shard * half_slots) + owner * half_slots + within % half_slots
    )
    update = jnp.take(joined, position, axis=1)
    return (grad_key, update)


def solution(mesh):
    return jax.shard_map(
        shards,
        mesh=mesh,
        in_specs=(
            P(("rep", "shard"), None),
            P(("rep", "shard"), None),
            P("shard", None, None),
            P("shard", None, None),
            P("shard", None, None),
            P(),
        ),
        out_specs=(P("shard", None), P("shard", None, None)),
        check_vma=False,
    )
```

profile of v0, /device:TPU:0, one launch (start us, length us, event | category | flops | bytes accessed | tf_op | source)
XLA Modules:
  0.0 247.9 jit_solution(18152596970215478150)
XLA Ops:
  8.0 0.0 copy-start
  8.0 0.0 reduce-scatter.2.cloned.1.call-start
  8.1 1.5 copy-done
  9.6 9.2 %fusion.9 = f32[4096,1024]{1,0:T(8,128)} fusion(bf16[256,4096]{1,0:T(8,128)(2,1)S(1)} %copy-done, bf16[256,1024]{1,0:T(8,128)(2,1)} %param.7), kind=kOutput, calls=%fused_computation.23 | convolution fusion | flops 2147483648 | bytes 19398656 | tf_op jit(solution)/shard_map/dot_general | solution.py:8
  18.8 0.0 reduce-scatter.2.cloned.1.call-update
  18.8 0.0 all-gather.2.cloned.1.call-start
  18.8 4.1 %fusion = bf16[512,2,512]{0,2,1:T(8,128)(2,1)} fusion(bf16[4,512,512]{2,1,0:T(8,128)(2,1)} %param.9, s32[]{:T(128)S(6)} %select_n.37, bf16[4,512,512]{2,1,0:T(8,128)(2,1)} %param.8, bf16[4,512,512]{2,1,0:T(8,128)(2,1)} %param.10), kind=kOutput, calls=%fused_computation.3 | convolution fusion | flops 1074790400 | bytes 4195840 | tf_op jit(solution)/shard_map/sij,sjk->isk/dot_general | solution.py:17
  22.9 2.5 %copy.14 = bf16[512,2,512]{2,1,0:T(2,128)(2,1)S(1)} copy(bf16[512,2,512]{0,2,1:T(8,128)(2,1)} %fusion) | data formatting | bytes 2097152 | tf_op jit(solution)/shard_map/convert_element_type | solution.py:19
  25.4 31.9 %all_to_all.18 = bf16[512,2,512]{2,1,0:T(2,128)(2,1)S(1)} all-to-all(bf16[512,2,512]{2,1,0:T(2,128)(2,1)S(1)} %copy.14), channel_id=1, replica_groups=mesh['rep'=2,'shard'=16] {'shard'}, dimensions={0} | all-to-all | bytes 2097152 | tf_op jit(solution)/shard_map/all_to_all | solution.py:37
  57.3 0.2 copy.15
  57.5 0.0 copy-start.1
  57.5 1.0 copy.16
  58.6 0.0 all-gather.2.cloned.1.call-update
  58.6 0.0 all-reduce.2.cloned.1.call-start
  58.6 140.4 %reduce-scatter.2.cloned.1.call-done = f32[256,1024]{1,0:T(8,128)} async-done(((f32[4096,1024]{1,0:T(8,128)}), f32[256,1024]{1,0:T(8,128)}) %reduce-scatter.2.cloned.1.call-update) | async-done | bytes 1048592 | tf_op jit(solution)/shard_map/reduce_scatter | solution.py:25
  199.0 0.0 all-reduce.2.cloned.1.call-update
  199.0 0.0 copy-done.1
  199.1 0.0 all-gather.2.cloned.1.call-done
  199.1 2.2 gather_fusion
  201.3 0.2 select_bitcast_fusion
  201.5 1.5 copy.17
  203.0 35.1 %all-reduce.2.cloned.1.call-done = f32[256,1024]{1,0:T(8,128)} async-done(((f32[256,1024]{1,0:T(8,128)}), f32[256,1024]{1,0:T(8,128)}) %all-reduce.2.cloned.1.call-update) | async-done | bytes 1048592 | tf_op jit(solution)/shard_map/psum | solution.py:28
  238.2 2.3 copy.20
  (2 shorter events, 0.0 us)
Async XLA Ops:
  8.0 1.6 copy-start
  8.0 191.0 %reduce-scatter.2.cloned.1.call-start = ((), (), s32[]{:S(2)}) async-start(), calls=%async_computation.2 | async-start | bytes 17825792 | tf_op jit(solution)/shard_map/reduce_scatter | solution.py:25
  18.8 180.3 %all-gather.2.cloned.1.call-start = ((), (), s32[]{:S(2)}) async-start(), calls=%async_computation.4 | async-start | bytes 3145728 | tf_op jit(solution)/shard_map/all_gather | solution.py:38
  57.5 141.5 %copy-start.1 = (s32[32]{0:T(128)S(1)}, s32[32]{0:T(128)}, u32[]{:S(2)}) copy-start(s32[32]{0:T(128)} %param.11) | copy-start | bytes 388
  58.6 179.6 %all-reduce.2.cloned.1.call-start = ((), (), s32[]{:S(2)}) async-start(), calls=%async_computation.3 | async-start | bytes 2097152 | tf_op jit(solution)/shard_map/psum | solution.py:28
Sparse Core Ops, SparseCore 0:
  18.9 180.0 reduce-scatter.1
Sparse Core Ops, SparseCore 1:
  58.7 33.3 all-gather.1
  199.1 39.0 all-reduce.1
where the time goes:
time: 248 us
  waiting for transfers between devices  176 us (71%)
  blocking collectives  31.9 us (13%)
  between operations  15.6 us (6%)
  matrix products  13.2 us (5%)
  local copies, waits for them, and re-layouts  11.3 us (5%)
    reduce_scatter x1, waiting for transfers between devices, shards(): lax.psum_scatter(column_term(tokens_x, key_grad), 'shard', scatter_dimens...  140 us
    psum x1, waiting for transfers between devices, shards(): grad_key = lax.psum(own_rows, 'rep')  35.1 us
    all_to_all x1, blocking collectives, shards(): lax.all_to_all(product, 'shard', split_axis=0, concat_axis=1, tiled=True)  31.9 us
    dot_general x1, matrix products, column_term(): lax.dot_general(features, cotangent, (((0,), (0,)), ((), ())), preferred_...  9.16 us
    unnamed x6, local copies, waits for them, and re-layouts  5.4 us
  transfers between devices with their start and end apart: 3, of which 2 were waited for; matrix products, arithmetic and copies ran while one was open for 5% of the time, Pallas kernels for 0%

commit v1 on v0

v1 whole, which is shorter than its diff:
```python
import functools
import math

import jax
import jax.numpy as jnp
from jax import lax
from jax.experimental import pallas as pl
from jax.experimental.pallas import tpu as pltpu
from jax.sharding import PartitionSpec as P


AXES = ("rep", "shard")
WIDE = 5
BF16, F32 = jnp.bfloat16, jnp.float32


def pick(value, index, axis):
    return lax.dynamic_index_in_dim(value, index, axis, keepdims=False)


def blocks_kernel(at, left, grads, right, *refs):
    *outs, held = refs
    n_out = len(outs)
    pair, _, group, _, half, order = left.shape
    rows = [left[p].reshape(n_out * group * half, order) for p in range(pair)]
    part = [
        jnp.dot(rows[p], grads[p], preferred_element_type=F32).astype(BF16) for p in range(pair)
    ]
    for p in range(pair):
        held[p] = jnp.dot(part[p], right[p], preferred_element_type=F32).astype(BF16)
    for k, out in enumerate(outs):
        first = pl.multiple_of((at[1] + k) % n_out * (group * half), group * half)
        for p in range(pair):
            out[p] = held[p, pl.ds(first, group * half), :].reshape(group, half, order)


def owned_blocks(at, left_root, slot_grads, right_root, n_shard):
    slots, order, _ = left_root.shape
    n_out, half = n_shard // 4, order // n_shard // 2
    if half % 16:
        own = pick(left_root.reshape(slots, n_shard, 2, half, order), at[0], 2)
        own = own.reshape(slots, n_shard * half, order)
        part = jnp.einsum("sij,sjk->sik", own, slot_grads, preferred_element_type=F32)
        full = jnp.einsum(
            "sij,sjk->sik", part.astype(BF16), right_root, preferred_element_type=F32
        ).astype(BF16)
        full = full.reshape(slots, n_out, 4, half, order)
        return [pick(full, (at[1] + k) % n_out, 1) for k in range(n_out)]
    pair = 2 if slots % 2 == 0 else 1
    square = pl.BlockSpec((pair, order, order), lambda s, at: (s, 0, 0))
    out_shape = jax.ShapeDtypeStruct((slots, 4, half, order), BF16)
    return pl.pallas_call(
        blocks_kernel,
        grid_spec=pltpu.PrefetchScalarGridSpec(
            num_scalar_prefetch=1,
            grid=(slots // pair,),
            in_specs=[
                pl.BlockSpec(
                    (pair, n_out, 4, 1, half, order), lambda s, at: (s, 0, 0, at[0], 0, 0)
                ),
                square,
                square,
            ],
            out_specs=[pl.BlockSpec((pair, 4, half, order), lambda s, at: (s, 0, 0, 0))] * n_out,
            scratch_shapes=[pltpu.VMEM((pair, n_shard * half, order), BF16)],
        ),
        out_shape=[out_shape] * n_out,
        compiler_params=pltpu.CompilerParams(vmem_limit_bytes=57 * 2**20),
        cost_estimate=pl.CostEstimate(
            flops=2 * slots * order**3, bytes_accessed=7 * slots * order**2, transcendentals=0
        ),
    )(at, left_root.reshape(slots, n_out, 4, 2, half, order), slot_grads, right_root)


def groups_of(n_out):
    cut = n_out // 2 + 1
    groups = [range(1, cut), range(cut, n_out), range(n_out, n_out + 1)]
    return [group for group in groups if len(group)]


def local_kernel(kernel, in_specs, out_specs, out_shape, scalars=0, flops=0, grid=(1,), scratch=()):
    moved = sum(2 * math.prod(shape.shape) * shape.dtype.itemsize for shape in out_shape)
    return pl.pallas_call(
        kernel,
        grid_spec=pltpu.PrefetchScalarGridSpec(
            num_scalar_prefetch=scalars,
            grid=grid,
            in_specs=in_specs,
            out_specs=out_specs,
            scratch_shapes=scratch,
        ),
        out_shape=out_shape,
        compiler_params=pltpu.CompilerParams(vmem_limit_bytes=16 * 2**20),
        cost_estimate=pl.CostEstimate(flops=flops + moved, bytes_accessed=moved, transcendentals=0),
    )


def grads_kernel(sizes, at, mine, other, key, other_key, sent_a, own_a, sent_b, own_b):
    n_out, start, wide, thin = sizes
    count, rows = sent_a.shape[1], sent_a.shape[3]
    o, y, c = at[1], at[2], at[3]
    base = 2 * wide
    for m in range(count):
        for near in (1, 0):
            row_group = y if near else 1 - y
            first = ((o + start + m) % n_out * 4 + row_group * 2 + c) * rows
            cols = pl.ds(pl.multiple_of(first, 128), rows)
            tile, other_tile = mine[:, cols], other[:, cols]

            def product(begin, size):
                kept = slice(begin, begin + size)
                return jnp.dot(key[kept, :], tile, preferred_element_type=F32) + jnp.dot(
                    other_key[kept, :], other_tile, preferred_element_type=F32
                )

            sent_a[near, m] = product(0, wide).astype(BF16)
            own_a[near, m] = product(wide, wide)
            out_b = own_b if near else sent_b
            out_b[0, m] = product(base, thin).astype(out_b.dtype)
            out_b[1, m] = product(base + thin, thin).astype(out_b.dtype)


def partial_rows(at, mine, other, key, other_key, n_shard, group, wide, thin):
    width, tok = key.shape
    n_out, rows = n_shard // 4, mine.shape[1] // n_shard
    count = len(group)
    if rows % 128:
        o, y, c = at[1], at[2], at[3]

        def select(tokens):
            cols = pick(tokens.reshape(tok, n_out, 2, 2, rows), c, 3)
            cols = jnp.stack([pick(cols, 1 - y, 2), pick(cols, y, 2)], 1)
            cols = jnp.concatenate([cols, cols], 2)
            return lax.dynamic_slice_in_dim(cols, o + group[0], count, 2)

        cols = jnp.concatenate([select(mine), select(other)], 0)
        keys = jnp.concatenate([key, other_key], 1)
        full = jnp.einsum("wt,tnkr->nkwr", keys, cols, preferred_element_type=F32)
        base = 2 * wide
        own_a, sent_a = full[:, :, wide:base], full[:, :, :wide]
        own_b = jnp.stack([full[1, :, base : base + thin], full[1, :, base + thin :]])
        sent_b = jnp.stack([full[0, :, base : base + thin], full[0, :, base + thin :]])
        return sent_a.astype(BF16), own_a, sent_b.astype(BF16), own_b
    vmem = pl.BlockSpec(memory_space=pltpu.VMEM)
    shape_a, shape_b = (2, count, wide, rows), (2, count, thin, rows)
    return local_kernel(
        functools.partial(grads_kernel, (n_out, group[0], wide, thin)),
        [vmem] * 4,
        [vmem] * 4,
        [
            jax.ShapeDtypeStruct(shape_a, BF16),
            jax.ShapeDtypeStruct(shape_a, F32),
            jax.ShapeDtypeStruct(shape_b, BF16),
            jax.ShapeDtypeStruct(shape_b, F32),
        ],
        scalars=1,
        flops=8 * tok * count * rows * width,
        grid=(),
    )(at, mine, other, key, other_key)


def fold_kernel(own, got, out):
    out[...] = (own[0] + got[0].astype(F32)).astype(BF16)


def folded(own, got):
    if own.shape[-1] % 128:
        return (own[0] + got[0].astype(F32)).astype(BF16)
    block = pl.BlockSpec((1,) + own.shape[1:], lambda i: (0, 0, 0, 0))
    return local_kernel(
        fold_kernel,
        [block, block],
        [pl.BlockSpec(own.shape[1:], lambda i: (0, 0, 0))],
        [jax.ShapeDtypeStruct(own.shape[1:], BF16)],
    )(own, got)[0]


def merge_kernel(own_a, got_a, last_a, own_b, got_b, last_b, *outs):
    wide = own_a.shape[2]
    for m, out in enumerate(outs):
        for part, own, got, last in (
            (slice(0, wide), own_a, got_a, last_a),
            (slice(wide, None), own_b, got_b, last_b),
        ):
            total = own[0, m] + got[0, m].astype(F32) + last[m].astype(F32)
            out[part, :] = total.astype(out.dtype)


def merged(own_a, got_a, last_a, own_b, got_b, last_b, types):
    count, wide, rows = own_a.shape[1:]
    thin = own_b.shape[2]
    if rows % 128:
        sum_a = own_a[1] + got_a[1].astype(F32) + last_a.astype(F32)
        sum_b = own_b[1] + got_b[1].astype(F32) + last_b.astype(F32)
        both = jnp.concatenate([sum_a, sum_b], 1)
        return [both[m].astype(dtype) for m, dtype in enumerate(types)]

    def specs(size):
        half = pl.BlockSpec((1, count, size, rows), lambda i: (1, 0, 0, 0))
        return [half, half, pl.BlockSpec((count, size, rows), lambda i: (0, 0, 0))]

    return local_kernel(
        merge_kernel,
        specs(wide) + specs(thin),
        [pl.BlockSpec((wide + thin, rows), lambda i: (0, 0))] * count,
        [jax.ShapeDtypeStruct((wide + thin, rows), dtype) for dtype in types],
    )(own_a, got_a, last_a, own_b, got_b, last_b)


def gather_kernel(at, *refs):
    *parts, out = refs
    for k, part in enumerate(parts):
        out[k] = part[...]


def row_sends(at, pieces):
    slots, _, half, order = pieces[0].shape
    if half % 16:
        return jnp.stack([lax.dynamic_slice_in_dim(p, (1 - at[2]) * 2, 2, 1) for p in pieces])
    part = (slots, 2, half, order)
    shape = (len(pieces),) + part
    return local_kernel(
        gather_kernel,
        [pl.BlockSpec(part, lambda i, at: (0, 1 - at[2], 0, 0))] * len(pieces),
        [pl.BlockSpec(shape, lambda i, at: (0, 0, 0, 0, 0))],
        [jax.ShapeDtypeStruct(shape, BF16)],
        scalars=1,
    )(at, *pieces)[0]


def core_kernel(at, *refs):
    *parts, row, near, far = refs
    c = at[3]
    for k, part in enumerate(parts):
        near[0, k], far[0, k] = part[:, c], part[:, 1 - c]
    near[1], far[1] = row[:, :, c], row[:, :, 1 - c]


def core_split(at, pieces, row):
    slots, _, half, order = pieces[0].shape
    n_out = len(pieces)
    if half % 16:
        own = jnp.stack([lax.dynamic_slice_in_dim(p, at[2] * 2, 2, 1) for p in pieces])
        both = jnp.stack([own, row])
        return pick(both, at[3], 3), pick(both, 1 - at[3], 3)
    shape = (2, n_out, slots, half, order)
    out = pl.BlockSpec(shape, lambda i, at: (0, 0, 0, 0, 0))
    return local_kernel(
        core_kernel,
        [pl.BlockSpec((slots, 2, half, order), lambda i, at: (0, at[2], 0, 0))] * n_out
        + [pl.BlockSpec(row.shape, lambda i, at: (0, 0, 0, 0, 0))],
        [out, out],
        [jax.ShapeDtypeStruct(shape, BF16)] * 2,
        scalars=1,
    )(at, *pieces, row)


def shards(tokens_x, key_grad, left_root, slot_grads, right_root, block_slot):
    n_rep, n_shard = lax.axis_size("rep"), lax.axis_size("shard")
    n_out = n_shard // 4
    x, s = lax.axis_index("rep"), lax.axis_index("shard")
    o, y, c = s // 4, s // 2 % 2, s % 2
    at = jnp.stack([x, o, y, c]).astype(jnp.int32)

    def permute(value, target):
        pairs = []
        for r in range(n_rep):
            for t in range(n_shard):
                r2, t2 = target(r, t)
                pairs.append((r * n_shard + t, r2 * n_shard + t2))
        return lax.ppermute(value, AXES, pairs)

    def swap_rep(value):
        return permute(value, lambda r, t: (1 - r, t))

    def swap_row(value):
        return permute(value, lambda r, t: (r, t ^ 2))

    def swap_core(value):
        return permute(value, lambda r, t: (r, t ^ 1))

    def shift_out(value, k):
        return permute(value, lambda r, t: (r, (t // 4 + k) % n_out * 4 + t % 4))

    width = key_grad.shape[1]
    wide = width * WIDE // 16
    thin = width // 2 - wide
    other_tokens = swap_core(tokens_x)
    key = key_grad.T
    low_a, high_a = key[:wide], key[wide : 2 * wide]
    low_b, high_b = key[2 * wide : 2 * wide + thin], key[2 * wide + thin :]
    key = jnp.where(
        x == 0,
        jnp.concatenate([high_a, low_a, high_b, low_b], 0),
        jnp.concatenate([low_a, high_a, low_b, high_b], 0),
    )
    other_key = swap_core(key)

    slots, order, _ = left_root.shape
    half = order // n_shard // 2
    pieces = owned_blocks(at, left_root, slot_grads, right_root, n_shard)
    by_out = [pieces[0]] + [shift_out(pieces[k], k) for k in range(1, n_out)]

    finished = []
    for group in groups_of(n_out):
        sent_a, own_a, sent_b, own_b = partial_rows(
            at, tokens_x, other_tokens, key, other_key, n_shard, group, wide, thin
        )
        got_a = swap_rep(sent_a)
        got_b = swap_row(sent_b)
        far_a = folded(own_a, got_a)
        far_b = folded(own_b, got_b)
        last_a = swap_row(far_a)
        last_b = swap_rep(far_b)
        sums = merged(
            own_a, got_a, last_a, own_b, got_b, last_b,
            [BF16 if k < n_out else F32 for k in group],
        )
        for k, piece in zip(group, sums):
            finished.append(shift_out(piece, k) if k < n_out else piece)

    sent_row = row_sends(at, by_out)
    got_row = swap_row(sent_row)
    near_core, far_core = core_split(at, by_out, got_row)
    held = jnp.stack([near_core, swap_core(far_core)])
    held = held.reshape(n_shard * slots, half, order)
    ids = jnp.arange(n_shard * slots, dtype=jnp.int32)
    source_out = (o - ids // slots % n_out + n_out) % n_out
    source_row = jnp.bitwise_xor(y, ids // (slots * n_out) % 2)
    source_core = jnp.bitwise_xor(c, ids // (slots * n_out * 2))
    slot_id = (source_out * 4 + source_row * 2 + source_core) * slots + ids % slots
    chosen = (block_slot[:, None] == slot_id[None, :]).astype(BF16)
    kept = jnp.einsum("bv,vhj->hbj", chosen, held, preferred_element_type=F32).astype(BF16)
    total = finished[-1]
    for piece in finished[:-1]:
        total = total + piece.astype(F32)
    done = lax.reduce_precision(total, 8, 7)
    far_done = swap_rep(done.astype(BF16)).astype(F32)
    low = jnp.where(x == 0, done, far_done)
    high = jnp.where(x == 0, far_done, done)
    grad_key = jnp.concatenate([low[:wide], high[:wide], low[wide:], high[wide:]], 0).T

    far_kept = swap_rep(kept)
    update = lax.dynamic_slice_in_dim(
        jnp.concatenate([kept, far_kept, kept], 0), x * half, 2 * half, 0
    )
    return (grad_key, update)


def solution(mesh):
    return jax.shard_map(
        shards,
        mesh=mesh,
        in_specs=(
            P(("rep", "shard"), None),
            P(("rep", "shard"), None),
            P("shard", None, None),
            P("shard", None, None),
            P("shard", None, None),
            P(),
        ),
        out_specs=(P("shard", None), P("shard", None, None)),
        check_vma=False,
    )
```

time: 248 us -> 117 us (0.47)
  waiting for transfers between devices: 176 us -> 62.9 us
  starting transfers between devices: 0.13 us -> 34.7 us
  blocking collectives: 31.9 us -> 0 us
  between operations: 15.6 us -> 0.9 us
  matrix products: 13.2 us -> 0.77 us
  Pallas kernels: 0 us -> 11 us
  local copies, waits for them, and re-layouts: 11.3 us -> 3.63 us
    reduce_scatter x1 -> x0, waiting for transfers between devices: 140 us -> none  [shards(): lax.psum_scatter(column_term(tokens_x, key_grad), 'shard', scatter_dimens...]
    ppermute x0 -> x24, waiting for transfers between devices: none -> 62.9 us  [permute(): return lax.ppermute(value, AXES, pairs)]
    psum x1 -> x0, waiting for transfers between devices: 35.1 us -> none  [shards(): grad_key = lax.psum(own_rows, 'rep')]
    ppermute x0 -> x24, starting transfers between devices: none -> 34.7 us  [permute(): return lax.ppermute(value, AXES, pairs)]
    all_to_all x1 -> x0, blocking collectives: 31.9 us -> none  [shards(): lax.all_to_all(product, 'shard', split_axis=0, concat_axis=1, tiled=True)]
    dot_general x2 -> x1, matrix products: 13.2 us -> 0.77 us  [shards(): jnp.einsum('bv,vhj->hbj', chosen, held, preferred_element_type=F32)]
    pallas_call x0 -> x15, Pallas kernels: none -> 11 us  [the longest x1 4.83 us: owned_blocks(): pl.pallas_call(blocks_kernel, grid_spec=pltpu.PrefetchScalarGridSpec(num_...]
    convert_element_type x1 -> x0, local copies, waits for them, and re-layouts: 2.5 us -> none  [precondition(): return jnp.einsum('sij,sjk->isk', left_part, right_block, preferred_eleme...]
  transfers between devices with their start and end apart: 3 -> 24, of which waited for: 2 -> 11; matrix products, arithmetic and copies ran while one was open for 5% -> 4% of each run, Pallas kernels for 0% -> 9%
where the time goes in v1:
time: 117 us
  waiting for transfers between devices  62.9 us (54%)
  starting transfers between devices  34.7 us (30%)
  Pallas kernels  11 us (9%)
  local copies, waits for them, and re-layouts  3.63 us (3%)
  other arithmetic  2.63 us (2%)
    ppermute x24, waiting for transfers between devices, permute(): return lax.ppermute(value, AXES, pairs)  62.9 us
    ppermute x24, starting transfers between devices, permute(): return lax.ppermute(value, AXES, pairs)  34.7 us
    pallas_call x1, Pallas kernels, owned_blocks(): pl.pallas_call(blocks_kernel, grid_spec=pltpu.PrefetchScalarGridSpec(num_...  4.83 us
    pallas_call x3, Pallas kernels, partial_rows(): local_kernel(functools.partial(grads_kernel, (n_out, group[0], wide, thin...  4.33 us
    unnamed x10, local copies, waits for them, and re-layouts  3.51 us
  transfers between devices with their start and end apart: 24, of which 11 were waited for; matrix products, arithmetic and copies ran while one was open for 4% of the time, Pallas kernels for 9%

profile of v1, /device:TPU:0, one launch (start us, length us, event | category | flops | bytes accessed | tf_op | source)
XLA Modules:
  0.0 116.5 jit_solution(8154921423367567681)
XLA Ops:
  0.6 0.6 collective-permute-start
  1.2 1.2 %copy.8 = bf16[256,1024]{0,1:T(8,128)(2,1)S(1)} copy(bf16[256,1024]{1,0:T(8,128)(2,1)} %param.7) | data formatting | bytes 1048576 | tf_op args[1]
  2.5 0.1 maximum_select_fusion.key
  2.7 0.6 pad_add_fusion.at
  3.4 4.8 %shard_map.89 = (bf16[4,4,16,512]{3,2,1,0:T(8,128)(2,1)}, bf16[4,4,16,512]{3,2,1,0:T(8,128)(2,1)}, bf16[4,4,16,512]{3,2,1,0:T(8,128)(2,1)}, bf16[4,4,16,512]{3,2,1,0:T(8,128)(2,1)}) custom-call(s32[4]{0:T(128)} %pad_add_fusion.at, bf16[4,4,4,2,16,512]{5,4,3,2,1,0:T(8,128)(2,1)} %bitcast.21, bf16[4,512,512]{2,1,0:T(8,128)(2,1)} %grads.1, ...), custom_call_target="tpu_custom_call" | custom-call | flops 1073741824 | bytes 7340032 | tf_op jit(solution)/shard_map/pallas_call | solution.py:52
  8.2 3.0 %collective-permute-start.18 = (bf16[4,4,16,512]{3,2,1,0:T(8,128)(2,1)}, bf16[4,4,16,512]{3,2,1,0:T(8,128)(2,1)S(1)}, u32[]{:S(2)}, u32[]{:S(2)}) collective-permute-start(bf16[4,4,16,512]{3,2,1,0:T(8,128)(2,1)} %get-tuple-element.37), channel_id=1, source_target_pairs={{0,4},{1,5},{2,6},{3,7},{4,8},{5,9},{6,10},{7,11},{8,12},{9,13},{1... | collective-permute-start | bytes 786440 | tf_op jit(solution)/shard_map/ppermute | solution.py:271
  11.2 2.6 %collective-permute-start.19 = (bf16[4,4,16,512]{3,2,1,0:T(8,128)(2,1)}, bf16[4,4,16,512]{3,2,1,0:T(8,128)(2,1)S(1)}, u32[]{:S(2)}, u32[]{:S(2)}) collective-permute-start(bf16[4,4,16,512]{3,2,1,0:T(8,128)(2,1)} %get-tuple-element.38), channel_id=1, source_target_pairs={{0,8},{1,9},{2,10},{3,11},{4,12},{5,13},{6,14},{7,15},{8,0},{9,1},... | collective-permute-start | bytes 786440 | tf_op jit(solution)/shard_map/ppermute | solution.py:271
  13.8 1.3 %collective-permute-start.20 = (bf16[4,4,16,512]{3,2,1,0:T(8,128)(2,1)}, bf16[4,4,16,512]{3,2,1,0:T(8,128)(2,1)S(1)}, u32[]{:S(2)}, u32[]{:S(2)}) collective-permute-start(bf16[4,4,16,512]{3,2,1,0:T(8,128)(2,1)} %get-tuple-element.39), channel_id=1, source_target_pairs={{0,12},{1,13},{2,14},{3,15},{4,0},{5,1},{6,2},{7,3},{8,4},{9,5},{1... | collective-permute-start | bytes 786440 | tf_op jit(solution)/shard_map/ppermute | solution.py:271
  15.2 5.6 %collective-permute-done.18.refs_1_ = bf16[4,4,16,512]{3,2,1,0:T(8,128)(2,1)S(1)} collective-permute-done((bf16[4,4,16,512]{3,2,1,0:T(8,128)(2,1)}, bf16[4,4,16,512]{3,2,1,0:T(8,128)(2,1)S(1)}, u32[]{:S(2)}, u32[]{:S(2)}) %collective-permute-start.18) | collective-permute-done | bytes 262176 | tf_op jit(solution)/shard_map/ppermute | solution.py:271
  20.7 10.6 %collective-permute-done.19.refs_2_ = bf16[4,4,16,512]{3,2,1,0:T(8,128)(2,1)S(1)} collective-permute-done((bf16[4,4,16,512]{3,2,1,0:T(8,128)(2,1)}, bf16[4,4,16,512]{3,2,1,0:T(8,128)(2,1)S(1)}, u32[]{:S(2)}, u32[]{:S(2)}) %collective-permute-start.19) | collective-permute-done | bytes 262176 | tf_op jit(solution)/shard_map/ppermute | solution.py:271
  31.4 0.9 copy-done.1
  32.3 0.6 shard_map.90
  32.9 1.6 %collective-permute-start.21 = (bf16[4,4,2,16,512]{4,3,2,1,0:T(8,128)(2,1)S(1)}, bf16[4,4,2,16,512]{4,3,2,1,0:T(8,128)(2,1)S(1)}, u32[]{:S(2)}, u32[]{:S(2)}) collective-permute-start(bf16[4,4,2,16,512]{4,3,2,1,0:T(8,128)(2,1)S(1)} %shard_map.90), channel_id=1, source_target_pairs={{0,2},{1,3},{2,0},{3,1},{4,6},{5,7},{6,4},{7,5},{8,10},{9,11},{10,... | collective-permute-start | bytes 1572872 | tf_op jit(solution)/shard_map/ppermute | solution.py:271
  34.5 1.8 %shard_map.81 = (bf16[2,2,320,256]{3,2,1,0:T(8,128)(2,1)S(1)}, f32[2,2,320,256]{3,2,1,0:T(8,128)S(1)}, bf16[2,2,192,256]{3,2,1,0:T(8,128)(2,1)S(1)}, f32[2,2,192,256]{3,2,1,0:T(8,128)S(1)}) custom-call(s32[4]{0:T(128)S(1)} %copy-done.2, bf16[256,4096]{1,0:T(8,128)(2,1)S(1)} %copy-done, bf16[256,4096]{1,0:T(8,128)(2,1)S(1)} %collective-permute-done.other, ...), custom_call_target="tpu_custom_call" | custom-call | flops 1080033280 | bytes 6291456 | tf_op jit(solution)/shard_map/pallas_call | solution.py:146
  36.3 1.6 %collective-permute-start.6 = (bf16[2,2,320,256]{3,2,1,0:T(8,128)(2,1)S(1)}, bf16[2,2,320,256]{3,2,1,0:T(8,128)(2,1)S(1)}, u32[]{:S(2)}, u32[]{:S(2)}) collective-permute-start(bf16[2,2,320,256]{3,2,1,0:T(8,128)(2,1)S(1)} %get-tuple-element.27), channel_id=1, source_target_pairs={{0,16},{1,17},{2,18},{3,19},{4,20},{5,21},{6,22},{7,23},{8,24},{9,... | collective-permute-start | bytes 1966088 | tf_op jit(solution)/shard_map/ppermute | solution.py:271
  37.9 8.8 %collective-permute-done.21.refs_4_ = bf16[4,4,2,16,512]{4,3,2,1,0:T(8,128)(2,1)S(1)} collective-permute-done((bf16[4,4,2,16,512]{4,3,2,1,0:T(8,128)(2,1)S(1)}, bf16[4,4,2,16,512]{4,3,2,1,0:T(8,128)(2,1)S(1)}, u32[]{:S(2)}, u32[]{:S(2)}) %collective-permute-start.21) | collective-permute-done | bytes 524320 | tf_op jit(solution)/shard_map/ppermute | solution.py:271
  46.7 0.6 shard_map.91
  47.4 1.6 %collective-permute-start.8 = (bf16[2,2,192,256]{3,2,1,0:T(8,128)(2,1)S(1)}, bf16[2,2,192,256]{3,2,1,0:T(8,128)(2,1)S(1)}, u32[]{:S(2)}, u32[]{:S(2)}) collective-permute-start(bf16[2,2,192,256]{3,2,1,0:T(8,128)(2,1)S(1)} %get-tuple-element.29), channel_id=1, source_target_pairs={{0,2},{1,3},{2,0},{3,1},{4,6},{5,7},{6,4},{7,5},{8,10},{9,11},{10,... | collective-permute-start | bytes 1179656 | tf_op jit(solution)/shard_map/ppermute | solution.py:271
  49.0 1.3 %shard_map.85 = (bf16[2,1,320,256]{3,2,1,0:T(8,128)(2,1)S(1)}, f32[2,1,320,256]{3,2,1,0:T(8,128)S(1)}, bf16[2,1,192,256]{3,2,1,0:T(8,128)(2,1)S(1)}, f32[2,1,192,256]{3,2,1,0:T(8,128)S(1)}) custom-call(s32[4]{0:T(128)S(1)} %copy-done.2, bf16[256,4096]{1,0:T(8,128)(2,1)S(1)} %copy-done, bf16[256,4096]{1,0:T(8,128)(2,1)S(1)} %collective-permute-done.other, ...), custom_call_target="tpu_custom_call" | custom-call | flops 540016640 | bytes 3145728 | tf_op jit(solution)/shard_map/pallas_call | solution.py:146
  50.3 1.6 %collective-permute-start.12 = (bf16[2,1,320,256]{3,2,1,0:T(8,128)(2,1)S(1)}, bf16[2,1,320,256]{3,2,1,0:T(8,128)(2,1)S(1)}, u32[]{:S(2)}, u32[]{:S(2)}) collective-permute-start(bf16[2,1,320,256]{3,2,1,0:T(8,128)(2,1)S(1)} %get-tuple-element.33), channel_id=1, source_target_pairs={{0,16},{1,17},{2,18},{3,19},{4,20},{5,21},{6,22},{7,23},{8,24},{9,... | collective-permute-start | bytes 983048 | tf_op jit(solution)/shard_map/ppermute | solution.py:271
  51.9 0.5 collective-permute-start.14
  52.4 1.3 %shard_map.77 = (bf16[2,1,320,256]{3,2,1,0:T(8,128)(2,1)S(1)}, f32[2,1,320,256]{3,2,1,0:T(8,128)S(1)}, bf16[2,1,192,256]{3,2,1,0:T(8,128)(2,1)S(1)}, f32[2,1,192,256]{3,2,1,0:T(8,128)S(1)}) custom-call(s32[4]{0:T(128)S(1)} %copy-done.2, bf16[256,4096]{1,0:T(8,128)(2,1)S(1)} %copy-done, bf16[256,4096]{1,0:T(8,128)(2,1)S(1)} %collective-permute-done.other, ...), custom_call_target="tpu_custom_call" | custom-call | flops 540016640 | bytes 3145728 | tf_op jit(solution)/shard_map/pallas_call | solution.py:146
  53.6 6.5 %collective-permute-done.12.got.got_a = bf16[2,1,320,256]{3,2,1,0:T(8,128)(2,1)S(1)} collective-permute-done((bf16[2,1,320,256]{3,2,1,0:T(8,128)(2,1)S(1)}, bf16[2,1,320,256]{3,2,1,0:T(8,128)(2,1)S(1)}, u32[]{:S(2)}, u32[]{:S(2)}) %collective-permute-start.12) | collective-permute-done | bytes 327712 | tf_op jit(solution)/shard_map/ppermute | solution.py:271
  60.1 0.5 collective-permute-start.4
  60.6 1.5 %collective-permute-start.2 = (bf16[2,1,320,256]{3,2,1,0:T(8,128)(2,1)S(1)}, bf16[2,1,320,256]{3,2,1,0:T(8,128)(2,1)S(1)}, u32[]{:S(2)}, u32[]{:S(2)}) collective-permute-start(bf16[2,1,320,256]{3,2,1,0:T(8,128)(2,1)S(1)} %get-tuple-element.23), channel_id=1, source_target_pairs={{0,16},{1,17},{2,18},{3,19},{4,20},{5,21},{6,22},{7,23},{8,24},{9,... | collective-permute-start | bytes 983048 | tf_op jit(solution)/shard_map/ppermute | solution.py:271
  62.2 1.6 %collective-permute-start.7 = (bf16[2,320,256]{2,1,0:T(8,128)(2,1)S(1)}, bf16[2,320,256]{2,1,0:T(8,128)(2,1)S(1)}, u32[]{:S(2)}, u32[]{:S(2)}) collective-permute-start(bf16[2,320,256]{2,1,0:T(8,128)(2,1)S(1)} %shard_map.82), channel_id=1, source_target_pairs={{0,2},{1,3},{2,0},{3,1},{4,6},{5,7},{6,4},{7,5},{8,10},{9,11},{10,... | collective-permute-start | bytes 983048 | tf_op jit(solution)/shard_map/ppermute | solution.py:271
  63.9 0.6 collective-permute-start.13
  64.5 0.7 collective-permute-start.9
  65.2 2.7 %collective-permute-done.4.got.got_b = bf16[2,1,192,256]{3,2,1,0:T(8,128)(2,1)S(1)} collective-permute-done((bf16[2,1,192,256]{3,2,1,0:T(8,128)(2,1)S(1)}, bf16[2,1,192,256]{3,2,1,0:T(8,128)(2,1)S(1)}, u32[]{:S(2)}, u32[]{:S(2)}) %collective-permute-start.4) | collective-permute-done | bytes 196640 | tf_op jit(solution)/shard_map/ppermute | solution.py:271
  67.9 1.5 %collective-permute-start.15 = (bf16[1,192,256]{2,1,0:T(8,128)(2,1)S(1)}, bf16[1,192,256]{2,1,0:T(8,128)(2,1)S(1)}, u32[]{:S(2)}, u32[]{:S(2)}) collective-permute-start(bf16[1,192,256]{2,1,0:T(8,128)(2,1)S(1)} %shard_map.87), channel_id=1, source_target_pairs={{0,16},{1,17},{2,18},{3,19},{4,20},{5,21},{6,22},{7,23},{8,24},{9,... | collective-permute-start | bytes 294920 | tf_op jit(solution)/shard_map/ppermute | solution.py:271
  69.4 0.1 pad_maximum_fusion
  69.5 1.7 %collective-permute-done.2.got.got_a = bf16[2,1,320,256]{3,2,1,0:T(8,128)(2,1)S(1)} collective-permute-done((bf16[2,1,320,256]{3,2,1,0:T(8,128)(2,1)S(1)}, bf16[2,1,320,256]{3,2,1,0:T(8,128)(2,1)S(1)}, u32[]{:S(2)}, u32[]{:S(2)}) %collective-permute-start.2) | collective-permute-done | bytes 327712 | tf_op jit(solution)/shard_map/ppermute | solution.py:271
  71.2 1.5 %collective-permute-start.5 = (bf16[1,192,256]{2,1,0:T(8,128)(2,1)S(1)}, bf16[1,192,256]{2,1,0:T(8,128)(2,1)S(1)}, u32[]{:S(2)}, u32[]{:S(2)}) collective-permute-start(bf16[1,192,256]{2,1,0:T(8,128)(2,1)S(1)} %shard_map.79), channel_id=1, source_target_pairs={{0,16},{1,17},{2,18},{3,19},{4,20},{5,21},{6,22},{7,23},{8,24},{9,... | collective-permute-start | bytes 294920 | tf_op jit(solution)/shard_map/ppermute | solution.py:271
  72.8 3.9 %collective-permute-done.15.last_b = bf16[1,192,256]{2,1,0:T(8,128)(2,1)S(1)} collective-permute-done((bf16[1,192,256]{2,1,0:T(8,128)(2,1)S(1)}, bf16[1,192,256]{2,1,0:T(8,128)(2,1)S(1)}, u32[]{:S(2)}, u32[]{:S(2)}) %collective-permute-start.15) | collective-permute-done | bytes 98336 | tf_op jit(solution)/shard_map/ppermute | solution.py:271
  76.6 1.5 %collective-permute-start.3 = (bf16[1,320,256]{2,1,0:T(8,128)(2,1)S(1)}, bf16[1,320,256]{2,1,0:T(8,128)(2,1)S(1)}, u32[]{:S(2)}, u32[]{:S(2)}) collective-permute-start(bf16[1,320,256]{2,1,0:T(8,128)(2,1)S(1)} %shard_map.78), channel_id=1, source_target_pairs={{0,2},{1,3},{2,0},{3,1},{4,6},{5,7},{6,4},{7,5},{8,10},{9,11},{10,... | collective-permute-start | bytes 491528 | tf_op jit(solution)/shard_map/ppermute | solution.py:271
  78.2 0.3 collective-permute-done.13.last_a
  78.6 6.4 %collective-permute-start.16 = (bf16[512,256]{1,0:T(8,128)(2,1)S(1)}, bf16[512,256]{1,0:T(8,128)(2,1)S(1)}, u32[]{:S(2)}, u32[]{:S(2)}) collective-permute-start(bf16[512,256]{1,0:T(8,128)(2,1)S(1)} %shard_map.88), channel_id=1, source_target_pairs={{0,12},{1,13},{2,14},{3,15},{4,0},{5,1},{6,2},{7,3},{8,4},{9,5},{1... | collective-permute-start | bytes 786440 | tf_op jit(solution)/shard_map/ppermute | solution.py:271
  85.0 0.2 shard_map.84
  85.2 1.3 %collective-permute-start.11 = (bf16[512,256]{1,0:T(8,128)(2,1)S(1)}, bf16[512,256]{1,0:T(8,128)(2,1)S(1)}, u32[]{:S(2)}, u32[]{:S(2)}) collective-permute-start(bf16[512,256]{1,0:T(8,128)(2,1)S(1)} %get-tuple-element.31), channel_id=1, source_target_pairs={{0,8},{1,9},{2,10},{3,11},{4,12},{5,13},{6,14},{7,15},{8,0},{9,1},... | collective-permute-start | bytes 786440 | tf_op jit(solution)/shard_map/ppermute | solution.py:271
  86.5 0.8 fusion
  87.3 1.6 %collective-permute-start.23 = (bf16[16,32,512]{2,1,0:T(8,128)(2,1)S(1)}, bf16[16,32,512]{2,1,0:T(8,128)(2,1)S(1)}, u32[]{:S(2)}, u32[]{:S(2)}) collective-permute-start(bf16[16,32,512]{2,1,0:T(8,128)(2,1)S(1)} %fusion), channel_id=1, source_target_pairs={{0,16},{1,17},{2,18},{3,19},{4,20},{5,21},{6,22},{7,23},{8,24},{9,... | collective-permute-start | bytes 1572872 | tf_op jit(solution)/shard_map/ppermute | solution.py:271
  88.9 2.8 %collective-permute-done.16 = bf16[512,256]{1,0:T(8,128)(2,1)S(1)} collective-permute-done((bf16[512,256]{1,0:T(8,128)(2,1)S(1)}, bf16[512,256]{1,0:T(8,128)(2,1)S(1)}, u32[]{:S(2)}, u32[]{:S(2)}) %collective-permute-start.16) | collective-permute-done | bytes 262176 | tf_op jit(solution)/shard_map/ppermute | solution.py:271
  91.7 16.6 %collective-permute-done.11 = bf16[512,256]{1,0:T(8,128)(2,1)S(1)} collective-permute-done((bf16[512,256]{1,0:T(8,128)(2,1)S(1)}, bf16[512,256]{1,0:T(8,128)(2,1)S(1)}, u32[]{:S(2)}, u32[]{:S(2)}) %collective-permute-start.11) | collective-permute-done | bytes 262176 | tf_op jit(solution)/shard_map/ppermute | solution.py:271
  108.3 0.1 fusion.22
  108.5 1.6 %collective-permute-start.17 = (bf16[512,256]{1,0:T(8,128)(2,1)S(1)}, bf16[512,256]{1,0:T(8,128)(2,1)S(1)}, u32[]{:S(2)}, u32[]{:S(2)}) collective-permute-start(bf16[512,256]{1,0:T(8,128)(2,1)S(1)} %get-tuple-element.44), channel_id=1, source_target_pairs={{0,16},{1,17},{2,18},{3,19},{4,20},{5,21},{6,22},{7,23},{8,24},{9,... | collective-permute-start | bytes 786440 | tf_op jit(solution)/shard_map/ppermute | solution.py:271
  110.0 1.5 %fusion.2 = bf16[32,32,512]{2,1,0:T(8,128)(2,1)} fusion(s32[]{:T(128)S(6)} %select_n.114, bf16[16,32,512]{2,1,0:T(8,128)(2,1)S(1)} %fusion, bf16[16,32,512]{2,1,0:T(8,128)(2,1)S(1)} %collective-permute-done.23), kind=kLoop, calls=%fused_computation.6 | loop fusion | flops 1048576 | bytes 2097156 | tf_op jit(solution)/shard_map/concatenate | solution.py:345
  111.5 3.4 %collective-permute-done.17 = bf16[512,256]{1,0:T(8,128)(2,1)S(1)} collective-permute-done((bf16[512,256]{1,0:T(8,128)(2,1)S(1)}, bf16[512,256]{1,0:T(8,128)(2,1)S(1)}, u32[]{:S(2)}, u32[]{:S(2)}) %collective-permute-start.17) | collective-permute-done | bytes 262176 | tf_op jit(solution)/shard_map/ppermute | solution.py:271
  115.2 1.3 %copy.10 = f32[256,1024]{1,0:T(8,128)} copy(f32[256,1024]{0,1:T(8,128)S(1)} %maximum_bitcast_fusion) | data formatting | bytes 2097152
  (40 shorter events, 0.9 us)
Async XLA Ops:
  0.6 33.9 %collective-permute-start = (bf16[256,4096]{1,0:T(8,128)(2,1)}, bf16[256,4096]{1,0:T(8,128)(2,1)S(1)}, u32[]{:S(2)}, u32[]{:S(2)}) collective-permute-start(bf16[256,4096]{1,0:T(8,128)(2,1)} %mine.5), channel_id=1, source_target_pairs={{0,1},{1,0},{2,3},{3,2},{4,5},{5,4},{6,7},{7,6},{8,9},{9,8},{10,11... | collective-permute-start | bytes 6291464 | tf_op jit(solution)/shard_map/ppermute | solution.py:271
  2.6 31.9 %collective-permute-start.1 = (bf16[1024,256]{1,0:T(8,128)(2,1)S(1)}, bf16[1024,256]{1,0:T(8,128)(2,1)S(1)}, u32[]{:S(2)}, u32[]{:S(2)}) collective-permute-start(bf16[1024,256]{1,0:T(8,128)(2,1)S(1)} %maximum_select_fusion.key), channel_id=1, source_target_pairs={{0,1},{1,0},{2,3},{3,2},{4,5},{5,4},{6,7},{7,6},{8,9},{9,8},{10,11... | collective-permute-start | bytes 1572872 | tf_op jit(solution)/shard_map/ppermute | solution.py:271
  3.4 28.0 %copy-start.2 = (s32[4]{0:T(128)S(1)}, s32[4]{0:T(128)}, u32[]{:S(2)}) copy-start(s32[4]{0:T(128)} %pad_add_fusion.at) | copy-start | bytes 52
  3.4 31.1 %copy-start = (bf16[256,4096]{1,0:T(8,128)(2,1)S(1)}, bf16[256,4096]{1,0:T(8,128)(2,1)}, u32[]{:S(2)}) copy-start(bf16[256,4096]{1,0:T(8,128)(2,1)} %mine.5) | copy-start | bytes 6291460
  8.2 12.5 %collective-permute-start.18 = (bf16[4,4,16,512]{3,2,1,0:T(8,128)(2,1)}, bf16[4,4,16,512]{3,2,1,0:T(8,128)(2,1)S(1)}, u32[]{:S(2)}, u32[]{:S(2)}) collective-permute-start(bf16[4,4,16,512]{3,2,1,0:T(8,128)(2,1)} %get-tuple-element.37), channel_id=1, source_target_pairs={{0,4},{1,5},{2,6},{3,7},{4,8},{5,9},{6,10},{7,11},{8,12},{9,13},{1... | collective-permute-start | bytes 786440 | tf_op jit(solution)/shard_map/ppermute | solution.py:271
  11.2 20.1 %collective-permute-start.19 = (bf16[4,4,16,512]{3,2,1,0:T(8,128)(2,1)}, bf16[4,4,16,512]{3,2,1,0:T(8,128)(2,1)S(1)}, u32[]{:S(2)}, u32[]{:S(2)}) collective-permute-start(bf16[4,4,16,512]{3,2,1,0:T(8,128)(2,1)} %get-tuple-element.38), channel_id=1, source_target_pairs={{0,8},{1,9},{2,10},{3,11},{4,12},{5,13},{6,14},{7,15},{8,0},{9,1},... | collective-permute-start | bytes 786440 | tf_op jit(solution)/shard_map/ppermute | solution.py:271
  13.8 17.5 %collective-permute-start.20 = (bf16[4,4,16,512]{3,2,1,0:T(8,128)(2,1)}, bf16[4,4,16,512]{3,2,1,0:T(8,128)(2,1)S(1)}, u32[]{:S(2)}, u32[]{:S(2)}) collective-permute-start(bf16[4,4,16,512]{3,2,1,0:T(8,128)(2,1)} %get-tuple-element.39), channel_id=1, source_target_pairs={{0,12},{1,13},{2,14},{3,15},{4,0},{5,1},{6,2},{7,3},{8,4},{9,5},{1... | collective-permute-start | bytes 786440 | tf_op jit(solution)/shard_map/ppermute | solution.py:271
  31.4 1.0 copy-start.1
  32.9 13.8 %collective-permute-start.21 = (bf16[4,4,2,16,512]{4,3,2,1,0:T(8,128)(2,1)S(1)}, bf16[4,4,2,16,512]{4,3,2,1,0:T(8,128)(2,1)S(1)}, u32[]{:S(2)}, u32[]{:S(2)}) collective-permute-start(bf16[4,4,2,16,512]{4,3,2,1,0:T(8,128)(2,1)S(1)} %shard_map.90), channel_id=1, source_target_pairs={{0,2},{1,3},{2,0},{3,1},{4,6},{5,7},{6,4},{7,5},{8,10},{9,11},{10,... | collective-permute-start | bytes 1572872 | tf_op jit(solution)/shard_map/ppermute | solution.py:271
  36.3 24.3 %collective-permute-start.6 = (bf16[2,2,320,256]{3,2,1,0:T(8,128)(2,1)S(1)}, bf16[2,2,320,256]{3,2,1,0:T(8,128)(2,1)S(1)}, u32[]{:S(2)}, u32[]{:S(2)}) collective-permute-start(bf16[2,2,320,256]{3,2,1,0:T(8,128)(2,1)S(1)} %get-tuple-element.27), channel_id=1, source_target_pairs={{0,16},{1,17},{2,18},{3,19},{4,20},{5,21},{6,22},{7,23},{8,24},{9,... | collective-permute-start | bytes 1966088 | tf_op jit(solution)/shard_map/ppermute | solution.py:271
  47.4 16.5 %collective-permute-start.22 = (bf16[2,4,4,16,512]{4,3,2,1,0:T(8,128)(2,1)S(1)}, bf16[2,4,4,16,512]{4,3,2,1,0:T(8,128)(2,1)S(1)}, u32[]{:S(2)}, u32[]{:S(2)}) collective-permute-start(bf16[2,4,4,16,512]{4,3,2,1,0:T(8,128)(2,1)S(1)} %get-tuple-element.41), channel_id=1, source_target_pairs={{0,1},{1,0},{2,3},{3,2},{4,5},{5,4},{6,7},{7,6},{8,9},{9,8},{10,11... | collective-permute-start | bytes 1572872 | tf_op jit(solution)/shard_map/ppermute | solution.py:271
  47.4 14.8 %collective-permute-start.8 = (bf16[2,2,192,256]{3,2,1,0:T(8,128)(2,1)S(1)}, bf16[2,2,192,256]{3,2,1,0:T(8,128)(2,1)S(1)}, u32[]{:S(2)}, u32[]{:S(2)}) collective-permute-start(bf16[2,2,192,256]{3,2,1,0:T(8,128)(2,1)S(1)} %get-tuple-element.29), channel_id=1, source_target_pairs={{0,2},{1,3},{2,0},{3,1},{4,6},{5,7},{6,4},{7,5},{8,10},{9,11},{10,... | collective-permute-start | bytes 1179656 | tf_op jit(solution)/shard_map/ppermute | solution.py:271
  50.3 9.8 %collective-permute-start.12 = (bf16[2,1,320,256]{3,2,1,0:T(8,128)(2,1)S(1)}, bf16[2,1,320,256]{3,2,1,0:T(8,128)(2,1)S(1)}, u32[]{:S(2)}, u32[]{:S(2)}) collective-permute-start(bf16[2,1,320,256]{3,2,1,0:T(8,128)(2,1)S(1)} %get-tuple-element.33), channel_id=1, source_target_pairs={{0,16},{1,17},{2,18},{3,19},{4,20},{5,21},{6,22},{7,23},{8,24},{9,... | collective-permute-start | bytes 983048 | tf_op jit(solution)/shard_map/ppermute | solution.py:271
  51.9 12.6 %collective-permute-start.14 = (bf16[2,1,192,256]{3,2,1,0:T(8,128)(2,1)S(1)}, bf16[2,1,192,256]{3,2,1,0:T(8,128)(2,1)S(1)}, u32[]{:S(2)}, u32[]{:S(2)}) collective-permute-start(bf16[2,1,192,256]{3,2,1,0:T(8,128)(2,1)S(1)} %get-tuple-element.35), channel_id=1, source_target_pairs={{0,2},{1,3},{2,0},{3,1},{4,6},{5,7},{6,4},{7,5},{8,10},{9,11},{10,... | collective-permute-start | bytes 589832 | tf_op jit(solution)/shard_map/ppermute | solution.py:271
  60.1 7.8 %collective-permute-start.4 = (bf16[2,1,192,256]{3,2,1,0:T(8,128)(2,1)S(1)}, bf16[2,1,192,256]{3,2,1,0:T(8,128)(2,1)S(1)}, u32[]{:S(2)}, u32[]{:S(2)}) collective-permute-start(bf16[2,1,192,256]{3,2,1,0:T(8,128)(2,1)S(1)} %get-tuple-element.25), channel_id=1, source_target_pairs={{0,2},{1,3},{2,0},{3,1},{4,6},{5,7},{6,4},{7,5},{8,10},{9,11},{10,... | collective-permute-start | bytes 589832 | tf_op jit(solution)/shard_map/ppermute | solution.py:271
  60.6 10.6 %collective-permute-start.2 = (bf16[2,1,320,256]{3,2,1,0:T(8,128)(2,1)S(1)}, bf16[2,1,320,256]{3,2,1,0:T(8,128)(2,1)S(1)}, u32[]{:S(2)}, u32[]{:S(2)}) collective-permute-start(bf16[2,1,320,256]{3,2,1,0:T(8,128)(2,1)S(1)} %get-tuple-element.23), channel_id=1, source_target_pairs={{0,16},{1,17},{2,18},{3,19},{4,20},{5,21},{6,22},{7,23},{8,24},{9,... | collective-permute-start | bytes 983048 | tf_op jit(solution)/shard_map/ppermute | solution.py:271
  62.2 22.8 %collective-permute-start.7 = (bf16[2,320,256]{2,1,0:T(8,128)(2,1)S(1)}, bf16[2,320,256]{2,1,0:T(8,128)(2,1)S(1)}, u32[]{:S(2)}, u32[]{:S(2)}) collective-permute-start(bf16[2,320,256]{2,1,0:T(8,128)(2,1)S(1)} %shard_map.82), channel_id=1, source_target_pairs={{0,2},{1,3},{2,0},{3,1},{4,6},{5,7},{6,4},{7,5},{8,10},{9,11},{10,... | collective-permute-start | bytes 983048 | tf_op jit(solution)/shard_map/ppermute | solution.py:271
  63.9 14.5 %collective-permute-start.13 = (bf16[1,320,256]{2,1,0:T(8,128)(2,1)S(1)}, bf16[1,320,256]{2,1,0:T(8,128)(2,1)S(1)}, u32[]{:S(2)}, u32[]{:S(2)}) collective-permute-start(bf16[1,320,256]{2,1,0:T(8,128)(2,1)S(1)} %shard_map.86), channel_id=1, source_target_pairs={{0,2},{1,3},{2,0},{3,1},{4,6},{5,7},{6,4},{7,5},{8,10},{9,11},{10,... | collective-permute-start | bytes 491528 | tf_op jit(solution)/shard_map/ppermute | solution.py:271
  64.5 20.5 %collective-permute-start.9 = (bf16[2,192,256]{2,1,0:T(8,128)(2,1)S(1)}, bf16[2,192,256]{2,1,0:T(8,128)(2,1)S(1)}, u32[]{:S(2)}, u32[]{:S(2)}) collective-permute-start(bf16[2,192,256]{2,1,0:T(8,128)(2,1)S(1)} %shard_map.83), channel_id=1, source_target_pairs={{0,16},{1,17},{2,18},{3,19},{4,20},{5,21},{6,22},{7,23},{8,24},{9,... | collective-permute-start | bytes 589832 | tf_op jit(solution)/shard_map/ppermute | solution.py:271
  67.9 8.7 %collective-permute-start.15 = (bf16[1,192,256]{2,1,0:T(8,128)(2,1)S(1)}, bf16[1,192,256]{2,1,0:T(8,128)(2,1)S(1)}, u32[]{:S(2)}, u32[]{:S(2)}) collective-permute-start(bf16[1,192,256]{2,1,0:T(8,128)(2,1)S(1)} %shard_map.87), channel_id=1, source_target_pairs={{0,16},{1,17},{2,18},{3,19},{4,20},{5,21},{6,22},{7,23},{8,24},{9,... | collective-permute-start | bytes 294920 | tf_op jit(solution)/shard_map/ppermute | solution.py:271
  71.2 16.1 %collective-permute-start.5 = (bf16[1,192,256]{2,1,0:T(8,128)(2,1)S(1)}, bf16[1,192,256]{2,1,0:T(8,128)(2,1)S(1)}, u32[]{:S(2)}, u32[]{:S(2)}) collective-permute-start(bf16[1,192,256]{2,1,0:T(8,128)(2,1)S(1)} %shard_map.79), channel_id=1, source_target_pairs={{0,16},{1,17},{2,18},{3,19},{4,20},{5,21},{6,22},{7,23},{8,24},{9,... | collective-permute-start | bytes 294920 | tf_op jit(solution)/shard_map/ppermute | solution.py:271
  76.6 12.2 %collective-permute-start.3 = (bf16[1,320,256]{2,1,0:T(8,128)(2,1)S(1)}, bf16[1,320,256]{2,1,0:T(8,128)(2,1)S(1)}, u32[]{:S(2)}, u32[]{:S(2)}) collective-permute-start(bf16[1,320,256]{2,1,0:T(8,128)(2,1)S(1)} %shard_map.78), channel_id=1, source_target_pairs={{0,2},{1,3},{2,0},{3,1},{4,6},{5,7},{6,4},{7,5},{8,10},{9,11},{10,... | collective-permute-start | bytes 491528 | tf_op jit(solution)/shard_map/ppermute | solution.py:271
  78.5 8.0 %copy-start.3 = (s32[32]{0:T(128)S(1)}, s32[32]{0:T(128)}, u32[]{:S(2)}) copy-start(s32[32]{0:T(128)} %param.11) | copy-start | bytes 388
  78.6 13.2 %collective-permute-start.16 = (bf16[512,256]{1,0:T(8,128)(2,1)S(1)}, bf16[512,256]{1,0:T(8,128)(2,1)S(1)}, u32[]{:S(2)}, u32[]{:S(2)}) collective-permute-start(bf16[512,256]{1,0:T(8,128)(2,1)S(1)} %shard_map.88), channel_id=1, source_target_pairs={{0,12},{1,13},{2,14},{3,15},{4,0},{5,1},{6,2},{7,3},{8,4},{9,5},{1... | collective-permute-start | bytes 786440 | tf_op jit(solution)/shard_map/ppermute | solution.py:271
  85.2 23.1 %collective-permute-start.11 = (bf16[512,256]{1,0:T(8,128)(2,1)S(1)}, bf16[512,256]{1,0:T(8,128)(2,1)S(1)}, u32[]{:S(2)}, u32[]{:S(2)}) collective-permute-start(bf16[512,256]{1,0:T(8,128)(2,1)S(1)} %get-tuple-element.31), channel_id=1, source_target_pairs={{0,8},{1,9},{2,10},{3,11},{4,12},{5,13},{6,14},{7,15},{8,0},{9,1},... | collective-permute-start | bytes 786440 | tf_op jit(solution)/shard_map/ppermute | solution.py:271
  86.5 21.8 %collective-permute-start.10 = (bf16[512,256]{1,0:T(8,128)(2,1)S(1)}, bf16[512,256]{1,0:T(8,128)(2,1)S(1)}, u32[]{:S(2)}, u32[]{:S(2)}) collective-permute-start(bf16[512,256]{1,0:T(8,128)(2,1)S(1)} %get-tuple-element.30), channel_id=1, source_target_pairs={{0,4},{1,5},{2,6},{3,7},{4,8},{5,9},{6,10},{7,11},{8,12},{9,13},{1... | collective-permute-start | bytes 786440 | tf_op jit(solution)/shard_map/ppermute | solution.py:271
  87.3 22.7 %collective-permute-start.23 = (bf16[16,32,512]{2,1,0:T(8,128)(2,1)S(1)}, bf16[16,32,512]{2,1,0:T(8,128)(2,1)S(1)}, u32[]{:S(2)}, u32[]{:S(2)}) collective-permute-start(bf16[16,32,512]{2,1,0:T(8,128)(2,1)S(1)} %fusion), channel_id=1, source_target_pairs={{0,16},{1,17},{2,18},{3,19},{4,20},{5,21},{6,22},{7,23},{8,24},{9,... | collective-permute-start | bytes 1572872 | tf_op jit(solution)/shard_map/ppermute | solution.py:271
  108.5 6.5 %collective-permute-start.17 = (bf16[512,256]{1,0:T(8,128)(2,1)S(1)}, bf16[512,256]{1,0:T(8,128)(2,1)S(1)}, u32[]{:S(2)}, u32[]{:S(2)}) collective-permute-start(bf16[512,256]{1,0:T(8,128)(2,1)S(1)} %get-tuple-element.44), channel_id=1, source_target_pairs={{0,16},{1,17},{2,18},{3,19},{4,20},{5,21},{6,22},{7,23},{8,24},{9,... | collective-permute-start | bytes 786440 | tf_op jit(solution)/shard_map/ppermute | solution.py:271

commit v2 on v1

--- a/solution.py
+++ b/solution.py
@@ -95,8 +95,9 @@
     )
 
 
-def grads_kernel(sizes, at, mine, other, key, other_key, sent_a, own_a, sent_b, own_b):
+def grads_kernel(sizes, at, mine, other, key, other_key, *outs):
     n_out, start, wide, thin = sizes
+    sent_a, own_a, *outs_b = outs
     count, rows = sent_a.shape[1], sent_a.shape[3]
     o, y, c = at[1], at[2], at[3]
     base = 2 * wide
@@ -113,14 +114,19 @@
                     other_key[kept, :], other_tile, preferred_element_type=F32
                 )
 
-            sent_a[near, m] = product(0, wide).astype(BF16)
-            own_a[near, m] = product(wide, wide)
-            out_b = own_b if near else sent_b
-            out_b[0, m] = product(base, thin).astype(out_b.dtype)
-            out_b[1, m] = product(base + thin, thin).astype(out_b.dtype)
-
-
-def partial_rows(at, mine, other, key, other_key, n_shard, group, wide, thin):
+            sent_a[near, m, :wide] = product(0, wide).astype(BF16)
+            own_a[near, m, :wide] = product(wide, wide)
+            far, close = product(base, thin), product(base + thin, thin)
+            if outs_b:
+                out_b = outs_b[near]
+                out_b[0, m] = far.astype(out_b.dtype)
+                out_b[1, m] = close.astype(out_b.dtype)
+            else:
+                sent_a[near, m, wide:] = far.astype(BF16)
+                own_a[near, m, wide:] = close
+
+
+def partial_rows(at, mine, other, key, other_key, n_shard, group, wide, thin, split):
     width, tok = key.shape
     n_out, rows = n_shard // 4, mine.shape[1] // n_shard
     count = len(group)
@@ -137,21 +143,23 @@
         keys = jnp.concatenate([key, other_key], 1)
         full = jnp.einsum("wt,tnkr->nkwr", keys, cols, preferred_element_type=F32)
         base = 2 * wide
-        own_a, sent_a = full[:, :, wide:base], full[:, :, :wide]
-        own_b = jnp.stack([full[1, :, base : base + thin], full[1, :, base + thin :]])
-        sent_b = jnp.stack([full[0, :, base : base + thin], full[0, :, base + thin :]])
+        far_b, near_b = full[:, :, base : base + thin], full[:, :, base + thin :]
+        sent_a, own_a = full[:, :, :wide], full[:, :, wide:base]
+        if not split:
+            sent_a = jnp.concatenate([sent_a, far_b], 2)
+            return sent_a.astype(BF16), jnp.concatenate([own_a, near_b], 2)
+        sent_b, own_b = (jnp.stack([far_b[n], near_b[n]]) for n in (0, 1))
         return sent_a.astype(BF16), own_a, sent_b.astype(BF16), own_b
     vmem = pl.BlockSpec(memory_space=pltpu.VMEM)
-    shape_a, shape_b = (2, count, wide, rows), (2, count, thin, rows)
+    heights = (wide, thin) if split else (wide + thin,)
     return local_kernel(
         functools.partial(grads_kernel, (n_out, group[0], wide, thin)),
         [vmem] * 4,
-        [vmem] * 4,
+        [vmem] * (2 * len(heights)),
         [
-            jax.ShapeDtypeStruct(shape_a, BF16),
-            jax.ShapeDtypeStruct(shape_a, F32),
-            jax.ShapeDtypeStruct(shape_b, BF16),
-            jax.ShapeDtypeStruct(shape_b, F32),
+            jax.ShapeDtypeStruct((2, count, height, rows), dtype)
+            for height in heights
+            for dtype in (BF16, F32)
         ],
         scalars=1,
         flops=8 * tok * count * rows * width,
@@ -175,84 +183,60 @@
     )(own, got)[0]
 
 
-def merge_kernel(own_a, got_a, last_a, own_b, got_b, last_b, *outs):
-    wide = own_a.shape[2]
-    for m, out in enumerate(outs):
-        for part, own, got, last in (
-            (slice(0, wide), own_a, got_a, last_a),
-            (slice(wide, None), own_b, got_b, last_b),
-        ):
+def merge_kernel(heights, *refs):
+    first = 0
+    for i, height in enumerate(heights):
+        own, got, last = refs[3 * i : 3 * i + 3]
+        for m, out in enumerate(refs[3 * len(heights) :]):
             total = own[0, m] + got[0, m].astype(F32) + last[m].astype(F32)
-            out[part, :] = total.astype(out.dtype)
-
-
-def merged(own_a, got_a, last_a, own_b, got_b, last_b, types):
-    count, wide, rows = own_a.shape[1:]
-    thin = own_b.shape[2]
+            out[first : first + height, :] = total.astype(out.dtype)
+        first += height
+
+
+def merged(parts, types):
+    count, rows = len(types), parts[0][0].shape[3]
+    heights = [own.shape[2] for own, _, _ in parts]
     if rows % 128:
-        sum_a = own_a[1] + got_a[1].astype(F32) + last_a.astype(F32)
-        sum_b = own_b[1] + got_b[1].astype(F32) + last_b.astype(F32)
-        both = jnp.concatenate([sum_a, sum_b], 1)
+        sums = [own[1] + got[1].astype(F32) + last.astype(F32) for own, got, last in parts]
+        both = jnp.concatenate(sums, 1)
         return [both[m].astype(dtype) for m, dtype in enumerate(types)]
-
-    def specs(size):
-        half = pl.BlockSpec((1, count, size, rows), lambda i: (1, 0, 0, 0))
-        return [half, half, pl.BlockSpec((count, size, rows), lambda i: (0, 0, 0))]
-
+    in_specs = []
+    for height in heights:
+        half = pl.BlockSpec((1, count, height, rows), lambda i: (1, 0, 0, 0))
+        in_specs += [half, half, pl.BlockSpec((count, height, rows), lambda i: (0, 0, 0))]
+    shape = (sum(heights), rows)
     return local_kernel(
-        merge_kernel,
-        specs(wide) + specs(thin),
-        [pl.BlockSpec((wide + thin, rows), lambda i: (0, 0))] * count,
-        [jax.ShapeDtypeStruct((wide + thin, rows), dtype) for dtype in types],
-    )(own_a, got_a, last_a, own_b, got_b, last_b)
-
-
-def gather_kernel(at, *refs):
-    *parts, out = refs
-    for k, part in enumerate(parts):
-        out[k] = part[...]
-
-
-def row_sends(at, pieces):
+        functools.partial(merge_kernel, heights),
+        in_specs,
+        [pl.BlockSpec(shape, lambda i: (0, 0))] * count,
+        [jax.ShapeDtypeStruct(shape, dtype) for dtype in types],
+    )(*(value for part in parts for value in part))
+
+
+def spread_kernel(at, *refs):
+    outs = refs[-4:]
+    y, c = at[2], at[3]
+    places = [row * 2 + core for core in (c, 1 - c) for row in (y, 1 - y)]
+    for k, piece in enumerate(refs[:-4]):
+        for place, out in zip(places, outs):
+            out[k] = piece[:, place]
+
+
+def spread(at, pieces):
     slots, _, half, order = pieces[0].shape
+    shape = (len(pieces), slots, half, order)
     if half % 16:
-        return jnp.stack([lax.dynamic_slice_in_dim(p, (1 - at[2]) * 2, 2, 1) for p in pieces])
-    part = (slots, 2, half, order)
-    shape = (len(pieces),) + part
+        both = jnp.stack(pieces)
+        places = [row * 2 + core for core in (at[3], 1 - at[3]) for row in (at[2], 1 - at[2])]
+        return [pick(both, place, 2) for place in places]
+    whole = pl.BlockSpec(pieces[0].shape, lambda i, at: (0, 0, 0, 0))
     return local_kernel(
-        gather_kernel,
-        [pl.BlockSpec(part, lambda i, at: (0, 1 - at[2], 0, 0))] * len(pieces),
-        [pl.BlockSpec(shape, lambda i, at: (0, 0, 0, 0, 0))],
-        [jax.ShapeDtypeStruct(shape, BF16)],
+        spread_kernel,
+        [whole] * len(pieces),
+        [pl.BlockSpec(shape, lambda i, at: (0, 0, 0, 0))] * 4,
+        [jax.ShapeDtypeStruct(shape, BF16)] * 4,
         scalars=1,
-    )(at, *pieces)[0]
-
-
-def core_kernel(at, *refs):
-    *parts, row, near, far = refs
-    c = at[3]
-    for k, part in enumerate(parts):
-        near[0, k], far[0, k] = part[:, c], part[:, 1 - c]
-    near[1], far[1] = row[:, :, c], row[:, :, 1 - c]
-
-
-def core_split(at, pieces, row):
-    slots, _, half, order = pieces[0].shape
-    n_out = len(pieces)
-    if half % 16:
-        own = jnp.stack([lax.dynamic_slice_in_dim(p, at[2] * 2, 2, 1) for p in pieces])
-        both = jnp.stack([own, row])
-        return pick(both, at[3], 3), pick(both, 1 - at[3], 3)
-    shape = (2, n_out, slots, half, order)
-    out = pl.BlockSpec(shape, lambda i, at: (0, 0, 0, 0, 0))
-    return local_kernel(
-        core_kernel,
-        [pl.BlockSpec((slots, 2, half, order), lambda i, at: (0, at[2], 0, 0))] * n_out
-        + [pl.BlockSpec(row.shape, lambda i, at: (0, 0, 0, 0, 0))],
-        [out, out],
-        [jax.ShapeDtypeStruct(shape, BF16)] * 2,
-        scalars=1,
-    )(at, *pieces, row)
+    )(at, *pieces)
 
 
 def shards(tokens_x, key_grad, left_root, slot_grads, right_root, block_slot):
@@ -303,26 +287,26 @@
 
     finished = []
     for group in groups_of(n_out):
-        sent_a, own_a, sent_b, own_b = partial_rows(
-            at, tokens_x, other_tokens, key, other_key, n_shard, group, wide, thin
+        kept = partial_rows(
+            at, tokens_x, other_tokens, key, other_key, n_shard, group, wide, thin,
+            group[-1] < n_out,
         )
-        got_a = swap_rep(sent_a)
-        got_b = swap_row(sent_b)
-        far_a = folded(own_a, got_a)
-        far_b = folded(own_b, got_b)
-        last_a = swap_row(far_a)
-        last_b = swap_rep(far_b)
-        sums = merged(
-            own_a, got_a, last_a, own_b, got_b, last_b,
-            [BF16 if k < n_out else F32 for k in group],
-        )
+        got_a = swap_rep(kept[0])
+        far_a = folded(kept[1], got_a)
+        parts = [(kept[1], got_a, swap_row(far_a))]
+        if len(kept) > 2:
+            got_b = swap_row(kept[2])
+            far_b = folded(kept[3], got_b)
+            parts.append((kept[3], got_b, swap_rep(far_b)))
+        sums = merged(parts, [BF16 if k < n_out else F32 for k in group])
         for k, piece in zip(group, sums):
             finished.append(shift_out(piece, k) if k < n_out else piece)
 
-    sent_row = row_sends(at, by_out)
-    got_row = swap_row(sent_row)
-    near_core, far_core = core_split(at, by_out, got_row)
-    held = jnp.stack([near_core, swap_core(far_core)])
+    own, far_row, far_core, far_both = spread(at, by_out)
+    far_row = swap_row(far_row)
+    far_core = swap_core(far_core)
+    far_both = permute(far_both, lambda r, t: (r, t ^ 3))
+    held = jnp.stack([own, far_row, far_core, far_both])
     held = held.reshape(n_shard * slots, half, order)
     ids = jnp.arange(n_shard * slots, dtype=jnp.int32)
     source_out = (o - ids // slots % n_out + n_out) % n_out

time: 117 us -> 109 us (0.932)
  waiting for transfers between devices: 62.9 us -> 59.1 us
  starting transfers between devices: 34.7 us -> 32.7 us
    ppermute x24 -> x23, waiting for transfers between devices: 62.9 us -> 59.1 us  [permute(): return lax.ppermute(value, AXES, pairs)]
    ppermute x24 -> x23, starting transfers between devices: 34.7 us -> 32.7 us  [permute(): return lax.ppermute(value, AXES, pairs)]
  transfers between devices with their start and end apart: 24 -> 23, of which waited for: 11 -> 12; matrix products, arithmetic and copies ran while one was open for 4% -> 4% of each run, Pallas kernels for 9% -> 9%
where the time goes in v2:
time: 109 us
  waiting for transfers between devices  59.1 us (54%)
  starting transfers between devices  32.7 us (30%)
  Pallas kernels  10.3 us (9%)
  local copies, waits for them, and re-layouts  2.68 us (2%)
  other arithmetic  2.64 us (2%)
    ppermute x23, waiting for transfers between devices, permute(): return lax.ppermute(value, AXES, pairs)  59.1 us
    ppermute x23, starting transfers between devices, permute(): return lax.ppermute(value, AXES, pairs)  32.7 us
    pallas_call x1, Pallas kernels, owned_blocks(): pl.pallas_call(blocks_kernel, grid_spec=pltpu.PrefetchScalarGridSpec(num_...  4.83 us
    pallas_call x3, Pallas kernels, partial_rows(): local_kernel(functools.partial(grads_kernel, (n_out, group[0], wide, thin...  4.34 us
    unnamed x10, local copies, waits for them, and re-layouts  2.57 us
  transfers between devices with their start and end apart: 23, of which 12 were waited for; matrix products, arithmetic and copies ran while one was open for 4% of the time, Pallas kernels for 9%

profile of v2, /device:TPU:0, one launch (start us, length us, event | category | flops | bytes accessed | tf_op | source)
XLA Modules:
  0.0 109.1 jit_solution(13506933469780106882)
XLA Ops:
  0.6 0.6 collective-permute-start
  1.2 1.2 %copy.8 = bf16[256,1024]{0,1:T(8,128)(2,1)S(1)} copy(bf16[256,1024]{1,0:T(8,128)(2,1)} %param.7) | data formatting | bytes 1048576 | tf_op args[1]
  2.5 0.1 maximum_select_fusion.key
  2.6 0.1 collective-permute-start.1
  2.7 0.6 pad_add_fusion.at
  3.4 4.8 %shard_map.88 = (bf16[4,4,16,512]{3,2,1,0:T(8,128)(2,1)}, bf16[4,4,16,512]{3,2,1,0:T(8,128)(2,1)}, bf16[4,4,16,512]{3,2,1,0:T(8,128)(2,1)}, bf16[4,4,16,512]{3,2,1,0:T(8,128)(2,1)}) custom-call(s32[4]{0:T(128)} %pad_add_fusion.at, bf16[4,4,4,2,16,512]{5,4,3,2,1,0:T(8,128)(2,1)} %bitcast.23, bf16[4,512,512]{2,1,0:T(8,128)(2,1)} %grads.1, ...), custom_call_target="tpu_custom_call" | custom-call | flops 1073741824 | bytes 7340032 | tf_op jit(solution)/shard_map/pallas_call | solution.py:52
  8.2 3.0 %collective-permute-start.16 = (bf16[4,4,16,512]{3,2,1,0:T(8,128)(2,1)}, bf16[4,4,16,512]{3,2,1,0:T(8,128)(2,1)S(1)}, u32[]{:S(2)}, u32[]{:S(2)}) collective-permute-start(bf16[4,4,16,512]{3,2,1,0:T(8,128)(2,1)} %get-tuple-element.35), channel_id=1, source_target_pairs={{0,4},{1,5},{2,6},{3,7},{4,8},{5,9},{6,10},{7,11},{8,12},{9,13},{1... | collective-permute-start | bytes 786440 | tf_op jit(solution)/shard_map/ppermute | solution.py:255
  11.2 2.6 %collective-permute-start.17 = (bf16[4,4,16,512]{3,2,1,0:T(8,128)(2,1)}, bf16[4,4,16,512]{3,2,1,0:T(8,128)(2,1)S(1)}, u32[]{:S(2)}, u32[]{:S(2)}) collective-permute-start(bf16[4,4,16,512]{3,2,1,0:T(8,128)(2,1)} %get-tuple-element.36), channel_id=1, source_target_pairs={{0,8},{1,9},{2,10},{3,11},{4,12},{5,13},{6,14},{7,15},{8,0},{9,1},... | collective-permute-start | bytes 786440 | tf_op jit(solution)/shard_map/ppermute | solution.py:255
  13.8 1.3 %collective-permute-start.18 = (bf16[4,4,16,512]{3,2,1,0:T(8,128)(2,1)}, bf16[4,4,16,512]{3,2,1,0:T(8,128)(2,1)S(1)}, u32[]{:S(2)}, u32[]{:S(2)}) collective-permute-start(bf16[4,4,16,512]{3,2,1,0:T(8,128)(2,1)} %get-tuple-element.37), channel_id=1, source_target_pairs={{0,12},{1,13},{2,14},{3,15},{4,0},{5,1},{6,2},{7,3},{8,4},{9,5},{1... | collective-permute-start | bytes 786440 | tf_op jit(solution)/shard_map/ppermute | solution.py:255
  15.2 1.8 %shard_map.80 = (bf16[2,2,320,256]{3,2,1,0:T(8,128)(2,1)S(1)}, f32[2,2,320,256]{3,2,1,0:T(8,128)S(1)}, bf16[2,2,192,256]{3,2,1,0:T(8,128)(2,1)S(1)}, f32[2,2,192,256]{3,2,1,0:T(8,128)S(1)}) custom-call(s32[4]{0:T(128)S(1)} %copy-done.2, bf16[256,4096]{1,0:T(8,128)(2,1)S(1)} %copy-done, bf16[256,4096]{1,0:T(8,128)(2,1)S(1)} %collective-permute-done.other, ...), custom_call_target="tpu_custom_call" | custom-call | flops 1080033280 | bytes 6291456 | tf_op jit(solution)/shard_map/pallas_call | solution.py:155
  17.0 1.6 %collective-permute-start.4 = (bf16[2,2,320,256]{3,2,1,0:T(8,128)(2,1)S(1)}, bf16[2,2,320,256]{3,2,1,0:T(8,128)(2,1)S(1)}, u32[]{:S(2)}, u32[]{:S(2)}) collective-permute-start(bf16[2,2,320,256]{3,2,1,0:T(8,128)(2,1)S(1)} %get-tuple-element.25), channel_id=1, source_target_pairs={{0,16},{1,17},{2,18},{3,19},{4,20},{5,21},{6,22},{7,23},{8,24},{9,... | collective-permute-start | bytes 1966088 | tf_op jit(solution)/shard_map/ppermute | solution.py:255
  18.5 2.2 %collective-permute-done.16.refs_1_ = bf16[4,4,16,512]{3,2,1,0:T(8,128)(2,1)S(1)} collective-permute-done((bf16[4,4,16,512]{3,2,1,0:T(8,128)(2,1)}, bf16[4,4,16,512]{3,2,1,0:T(8,128)(2,1)S(1)}, u32[]{:S(2)}, u32[]{:S(2)}) %collective-permute-start.16) | collective-permute-done | bytes 262176 | tf_op jit(solution)/shard_map/ppermute | solution.py:255
  20.7 10.6 %collective-permute-done.17.refs_2_ = bf16[4,4,16,512]{3,2,1,0:T(8,128)(2,1)S(1)} collective-permute-done((bf16[4,4,16,512]{3,2,1,0:T(8,128)(2,1)}, bf16[4,4,16,512]{3,2,1,0:T(8,128)(2,1)S(1)}, u32[]{:S(2)}, u32[]{:S(2)}) %collective-permute-start.17) | collective-permute-done | bytes 262176 | tf_op jit(solution)/shard_map/ppermute | solution.py:255
  31.3 0.6 shard_map.89
  32.0 1.1 %collective-permute-start.21 = (bf16[4,4,16,512]{3,2,1,0:T(8,128)(2,1)S(1)}, bf16[4,4,16,512]{3,2,1,0:T(8,128)(2,1)S(1)}, u32[]{:S(2)}, u32[]{:S(2)}) collective-permute-start(bf16[4,4,16,512]{3,2,1,0:T(8,128)(2,1)S(1)} %get-tuple-element.41), channel_id=1, source_target_pairs={{0,3},{1,2},{2,1},{3,0},{4,7},{5,6},{6,5},{7,4},{8,11},{9,10},{10,... | collective-permute-start | bytes 786440 | tf_op jit(solution)/shard_map/ppermute | solution.py:255
  33.1 1.3 %shard_map.84 = (bf16[2,1,320,256]{3,2,1,0:T(8,128)(2,1)S(1)}, f32[2,1,320,256]{3,2,1,0:T(8,128)S(1)}, bf16[2,1,192,256]{3,2,1,0:T(8,128)(2,1)S(1)}, f32[2,1,192,256]{3,2,1,0:T(8,128)S(1)}) custom-call(s32[4]{0:T(128)S(1)} %copy-done.2, bf16[256,4096]{1,0:T(8,128)(2,1)S(1)} %copy-done, bf16[256,4096]{1,0:T(8,128)(2,1)S(1)} %collective-permute-done.other, ...), custom_call_target="tpu_custom_call" | custom-call | flops 540016640 | bytes 3145728 | tf_op jit(solution)/shard_map/pallas_call | solution.py:155
  34.3 1.6 %collective-permute-start.10 = (bf16[2,1,320,256]{3,2,1,0:T(8,128)(2,1)S(1)}, bf16[2,1,320,256]{3,2,1,0:T(8,128)(2,1)S(1)}, u32[]{:S(2)}, u32[]{:S(2)}) collective-permute-start(bf16[2,1,320,256]{3,2,1,0:T(8,128)(2,1)S(1)} %get-tuple-element.31), channel_id=1, source_target_pairs={{0,16},{1,17},{2,18},{3,19},{4,20},{5,21},{6,22},{7,23},{8,24},{9,... | collective-permute-start | bytes 983048 | tf_op jit(solution)/shard_map/ppermute | solution.py:255
  35.9 0.5 collective-permute-start.6
  36.4 1.3 %shard_map.77 = (bf16[2,1,512,256]{3,2,1,0:T(8,128)(2,1)S(1)}, f32[2,1,512,256]{3,2,1,0:T(8,128)S(1)}) custom-call(s32[4]{0:T(128)S(1)} %copy-done.2, bf16[256,4096]{1,0:T(8,128)(2,1)S(1)} %copy-done, bf16[256,4096]{1,0:T(8,128)(2,1)S(1)} %collective-permute-done.other, bf16[1024,256]{1,0:T(8,128)(2,1)S(1)} %maximum_select_fusion.key, ...), custom_call_target="tpu_custom_call" | custom-call | flops 540016640 | bytes 3145728 | tf_op jit(solution)/shard_map/pallas_call | solution.py:155
  37.7 0.6 collective-permute-start.2
  38.3 2.3 %collective-permute-done.21 = bf16[4,4,16,512]{3,2,1,0:T(8,128)(2,1)S(1)} collective-permute-done((bf16[4,4,16,512]{3,2,1,0:T(8,128)(2,1)S(1)}, bf16[4,4,16,512]{3,2,1,0:T(8,128)(2,1)S(1)}, u32[]{:S(2)}, u32[]{:S(2)}) %collective-permute-start.21) | collective-permute-done | bytes 262176 | tf_op jit(solution)/shard_map/ppermute | solution.py:255
  40.5 0.3 collective-permute-start.20
  40.9 4.1 %collective-permute-done.10.got.refs_1_ = bf16[2,1,320,256]{3,2,1,0:T(8,128)(2,1)S(1)} collective-permute-done((bf16[2,1,320,256]{3,2,1,0:T(8,128)(2,1)S(1)}, bf16[2,1,320,256]{3,2,1,0:T(8,128)(2,1)S(1)}, u32[]{:S(2)}, u32[]{:S(2)}) %collective-permute-start.10) | collective-permute-done | bytes 327712 | tf_op jit(solution)/shard_map/ppermute | solution.py:255
  45.0 0.5 collective-permute-start.12
  45.5 1.5 %collective-permute-start.19 = (bf16[4,4,16,512]{3,2,1,0:T(8,128)(2,1)S(1)}, bf16[4,4,16,512]{3,2,1,0:T(8,128)(2,1)S(1)}, u32[]{:S(2)}, u32[]{:S(2)}) collective-permute-start(bf16[4,4,16,512]{3,2,1,0:T(8,128)(2,1)S(1)} %get-tuple-element.39), channel_id=1, source_target_pairs={{0,2},{1,3},{2,0},{3,1},{4,6},{5,7},{6,4},{7,5},{8,10},{9,11},{10,... | collective-permute-start | bytes 786440 | tf_op jit(solution)/shard_map/ppermute | solution.py:255
  47.1 2.0 %collective-permute-done.6.got.refs_4_ = bf16[2,2,192,256]{3,2,1,0:T(8,128)(2,1)S(1)} collective-permute-done((bf16[2,2,192,256]{3,2,1,0:T(8,128)(2,1)S(1)}, bf16[2,2,192,256]{3,2,1,0:T(8,128)(2,1)S(1)}, u32[]{:S(2)}, u32[]{:S(2)}) %collective-permute-start.6) | collective-permute-done | bytes 393248 | tf_op jit(solution)/shard_map/ppermute | solution.py:255
  49.2 1.5 %collective-permute-start.5 = (bf16[2,320,256]{2,1,0:T(8,128)(2,1)S(1)}, bf16[2,320,256]{2,1,0:T(8,128)(2,1)S(1)}, u32[]{:S(2)}, u32[]{:S(2)}) collective-permute-start(bf16[2,320,256]{2,1,0:T(8,128)(2,1)S(1)} %shard_map.81), channel_id=1, source_target_pairs={{0,2},{1,3},{2,0},{3,1},{4,6},{5,7},{6,4},{7,5},{8,10},{9,11},{10,... | collective-permute-start | bytes 983048 | tf_op jit(solution)/shard_map/ppermute | solution.py:255
  50.8 0.6 collective-permute-start.11
  51.4 2.0 %collective-permute-done.12.got.refs_4_ = bf16[2,1,192,256]{3,2,1,0:T(8,128)(2,1)S(1)} collective-permute-done((bf16[2,1,192,256]{3,2,1,0:T(8,128)(2,1)S(1)}, bf16[2,1,192,256]{3,2,1,0:T(8,128)(2,1)S(1)}, u32[]{:S(2)}, u32[]{:S(2)}) %collective-permute-start.12) | collective-permute-done | bytes 196640 | tf_op jit(solution)/shard_map/ppermute | solution.py:255
  53.4 1.5 %collective-permute-start.7 = (bf16[2,192,256]{2,1,0:T(8,128)(2,1)S(1)}, bf16[2,192,256]{2,1,0:T(8,128)(2,1)S(1)}, u32[]{:S(2)}, u32[]{:S(2)}) collective-permute-start(bf16[2,192,256]{2,1,0:T(8,128)(2,1)S(1)} %shard_map.82), channel_id=1, source_target_pairs={{0,16},{1,17},{2,18},{3,19},{4,20},{5,21},{6,22},{7,23},{8,24},{9,... | collective-permute-start | bytes 589832 | tf_op jit(solution)/shard_map/ppermute | solution.py:255
  54.9 4.1 %collective-permute-done.19 = bf16[4,4,16,512]{3,2,1,0:T(8,128)(2,1)S(1)} collective-permute-done((bf16[4,4,16,512]{3,2,1,0:T(8,128)(2,1)S(1)}, bf16[4,4,16,512]{3,2,1,0:T(8,128)(2,1)S(1)}, u32[]{:S(2)}, u32[]{:S(2)}) %collective-permute-start.19) | collective-permute-done | bytes 262176 | tf_op jit(solution)/shard_map/ppermute | solution.py:255
  59.0 1.5 %collective-permute-start.13 = (bf16[1,192,256]{2,1,0:T(8,128)(2,1)S(1)}, bf16[1,192,256]{2,1,0:T(8,128)(2,1)S(1)}, u32[]{:S(2)}, u32[]{:S(2)}) collective-permute-start(bf16[1,192,256]{2,1,0:T(8,128)(2,1)S(1)} %shard_map.86), channel_id=1, source_target_pairs={{0,16},{1,17},{2,18},{3,19},{4,20},{5,21},{6,22},{7,23},{8,24},{9,... | collective-permute-start | bytes 294920 | tf_op jit(solution)/shard_map/ppermute | solution.py:255
  60.5 0.1 pad_maximum_fusion
  60.6 3.0 %collective-permute-done.13.refs_5_ = bf16[1,192,256]{2,1,0:T(8,128)(2,1)S(1)} collective-permute-done((bf16[1,192,256]{2,1,0:T(8,128)(2,1)S(1)}, bf16[1,192,256]{2,1,0:T(8,128)(2,1)S(1)}, u32[]{:S(2)}, u32[]{:S(2)}) %collective-permute-start.13) | collective-permute-done | bytes 98336 | tf_op jit(solution)/shard_map/ppermute | solution.py:255
  63.6 5.8 %collective-permute-done.11.refs_2_ = bf16[1,320,256]{2,1,0:T(8,128)(2,1)S(1)} collective-permute-done((bf16[1,320,256]{2,1,0:T(8,128)(2,1)S(1)}, bf16[1,320,256]{2,1,0:T(8,128)(2,1)S(1)}, u32[]{:S(2)}, u32[]{:S(2)}) %collective-permute-start.11) | collective-permute-done | bytes 163872 | tf_op jit(solution)/shard_map/ppermute | solution.py:255
  69.5 7.2 %collective-permute-start.14 = (bf16[512,256]{1,0:T(8,128)(2,1)S(1)}, bf16[512,256]{1,0:T(8,128)(2,1)S(1)}, u32[]{:S(2)}, u32[]{:S(2)}) collective-permute-start(bf16[512,256]{1,0:T(8,128)(2,1)S(1)} %shard_map.87), channel_id=1, source_target_pairs={{0,12},{1,13},{2,14},{3,15},{4,0},{5,1},{6,2},{7,3},{8,4},{9,5},{1... | collective-permute-start | bytes 786440 | tf_op jit(solution)/shard_map/ppermute | solution.py:255
  76.7 0.3 collective-permute-start.3
  77.1 0.2 shard_map.83
  77.3 1.7 %collective-permute-start.9 = (bf16[512,256]{1,0:T(8,128)(2,1)S(1)}, bf16[512,256]{1,0:T(8,128)(2,1)S(1)}, u32[]{:S(2)}, u32[]{:S(2)}) collective-permute-start(bf16[512,256]{1,0:T(8,128)(2,1)S(1)} %get-tuple-element.29), channel_id=1, source_target_pairs={{0,8},{1,9},{2,10},{3,11},{4,12},{5,13},{6,14},{7,15},{8,0},{9,1},... | collective-permute-start | bytes 786440 | tf_op jit(solution)/shard_map/ppermute | solution.py:255
  79.0 0.8 fusion
  79.8 1.6 %collective-permute-start.22 = (bf16[16,32,512]{2,1,0:T(8,128)(2,1)S(1)}, bf16[16,32,512]{2,1,0:T(8,128)(2,1)S(1)}, u32[]{:S(2)}, u32[]{:S(2)}) collective-permute-start(bf16[16,32,512]{2,1,0:T(8,128)(2,1)S(1)} %fusion), channel_id=1, source_target_pairs={{0,16},{1,17},{2,18},{3,19},{4,20},{5,21},{6,22},{7,23},{8,24},{9,... | collective-permute-start | bytes 1572872 | tf_op jit(solution)/shard_map/ppermute | solution.py:255
  81.4 3.4 %collective-permute-done.3.refs_2_ = bf16[1,512,256]{2,1,0:T(8,128)(2,1)S(1)} collective-permute-done((bf16[1,512,256]{2,1,0:T(8,128)(2,1)S(1)}, bf16[1,512,256]{2,1,0:T(8,128)(2,1)S(1)}, u32[]{:S(2)}, u32[]{:S(2)}) %collective-permute-start.3) | collective-permute-done | bytes 262176 | tf_op jit(solution)/shard_map/ppermute | solution.py:255
  84.9 15.2 %collective-permute-done.9 = bf16[512,256]{1,0:T(8,128)(2,1)S(1)} collective-permute-done((bf16[512,256]{1,0:T(8,128)(2,1)S(1)}, bf16[512,256]{1,0:T(8,128)(2,1)S(1)}, u32[]{:S(2)}, u32[]{:S(2)}) %collective-permute-start.9) | collective-permute-done | bytes 262176 | tf_op jit(solution)/shard_map/ppermute | solution.py:255
  100.1 0.1 fusion.22
  100.2 1.6 %collective-permute-start.15 = (bf16[512,256]{1,0:T(8,128)(2,1)S(1)}, bf16[512,256]{1,0:T(8,128)(2,1)S(1)}, u32[]{:S(2)}, u32[]{:S(2)}) collective-permute-start(bf16[512,256]{1,0:T(8,128)(2,1)S(1)} %get-tuple-element.44), channel_id=1, source_target_pairs={{0,16},{1,17},{2,18},{3,19},{4,20},{5,21},{6,22},{7,23},{8,24},{9,... | collective-permute-start | bytes 786440 | tf_op jit(solution)/shard_map/ppermute | solution.py:255
  101.8 1.5 %fusion.2 = bf16[32,32,512]{2,1,0:T(8,128)(2,1)} fusion(s32[]{:T(128)S(6)} %select_n.114, bf16[16,32,512]{2,1,0:T(8,128)(2,1)S(1)} %fusion, bf16[16,32,512]{2,1,0:T(8,128)(2,1)S(1)} %collective-permute-done.22), kind=kLoop, calls=%fused_computation.6 | loop fusion | flops 1048576 | bytes 2097156 | tf_op jit(solution)/shard_map/concatenate | solution.py:329
  103.3 4.3 %collective-permute-done.15 = bf16[512,256]{1,0:T(8,128)(2,1)S(1)} collective-permute-done((bf16[512,256]{1,0:T(8,128)(2,1)S(1)}, bf16[512,256]{1,0:T(8,128)(2,1)S(1)}, u32[]{:S(2)}, u32[]{:S(2)}) %collective-permute-start.15) | collective-permute-done | bytes 262176 | tf_op jit(solution)/shard_map/ppermute | solution.py:255
  107.8 1.3 %copy.10 = f32[256,1024]{1,0:T(8,128)} copy(f32[256,1024]{0,1:T(8,128)S(1)} %maximum_bitcast_fusion) | data formatting | bytes 2097152
  (36 shorter events, 0.7 us)
Async XLA Ops:
  0.6 14.5 %collective-permute-start = (bf16[256,4096]{1,0:T(8,128)(2,1)}, bf16[256,4096]{1,0:T(8,128)(2,1)S(1)}, u32[]{:S(2)}, u32[]{:S(2)}) collective-permute-start(bf16[256,4096]{1,0:T(8,128)(2,1)} %mine.5), channel_id=1, source_target_pairs={{0,1},{1,0},{2,3},{3,2},{4,5},{5,4},{6,7},{7,6},{8,9},{9,8},{10,11... | collective-permute-start | bytes 6291464 | tf_op jit(solution)/shard_map/ppermute | solution.py:255
  2.6 12.5 %collective-permute-start.1 = (bf16[1024,256]{1,0:T(8,128)(2,1)S(1)}, bf16[1024,256]{1,0:T(8,128)(2,1)S(1)}, u32[]{:S(2)}, u32[]{:S(2)}) collective-permute-start(bf16[1024,256]{1,0:T(8,128)(2,1)S(1)} %maximum_select_fusion.key), channel_id=1, source_target_pairs={{0,1},{1,0},{2,3},{3,2},{4,5},{5,4},{6,7},{7,6},{8,9},{9,8},{10,11... | collective-permute-start | bytes 1572872 | tf_op jit(solution)/shard_map/ppermute | solution.py:255
  3.4 11.8 %copy-start = (bf16[256,4096]{1,0:T(8,128)(2,1)S(1)}, bf16[256,4096]{1,0:T(8,128)(2,1)}, u32[]{:S(2)}) copy-start(bf16[256,4096]{1,0:T(8,128)(2,1)} %mine.5) | copy-start | bytes 6291460
  3.4 11.8 %copy-start.2 = (s32[4]{0:T(128)S(1)}, s32[4]{0:T(128)}, u32[]{:S(2)}) copy-start(s32[4]{0:T(128)} %pad_add_fusion.at) | copy-start | bytes 52
  8.2 12.5 %collective-permute-start.16 = (bf16[4,4,16,512]{3,2,1,0:T(8,128)(2,1)}, bf16[4,4,16,512]{3,2,1,0:T(8,128)(2,1)S(1)}, u32[]{:S(2)}, u32[]{:S(2)}) collective-permute-start(bf16[4,4,16,512]{3,2,1,0:T(8,128)(2,1)} %get-tuple-element.35), channel_id=1, source_target_pairs={{0,4},{1,5},{2,6},{3,7},{4,8},{5,9},{6,10},{7,11},{8,12},{9,13},{1... | collective-permute-start | bytes 786440 | tf_op jit(solution)/shard_map/ppermute | solution.py:255
  11.2 20.1 %collective-permute-start.17 = (bf16[4,4,16,512]{3,2,1,0:T(8,128)(2,1)}, bf16[4,4,16,512]{3,2,1,0:T(8,128)(2,1)S(1)}, u32[]{:S(2)}, u32[]{:S(2)}) collective-permute-start(bf16[4,4,16,512]{3,2,1,0:T(8,128)(2,1)} %get-tuple-element.36), channel_id=1, source_target_pairs={{0,8},{1,9},{2,10},{3,11},{4,12},{5,13},{6,14},{7,15},{8,0},{9,1},... | collective-permute-start | bytes 786440 | tf_op jit(solution)/shard_map/ppermute | solution.py:255
  13.8 17.5 %copy-start.1 = (bf16[4,4,16,512]{3,2,1,0:T(8,128)(2,1)S(1)}, bf16[4,4,16,512]{3,2,1,0:T(8,128)(2,1)}, u32[]{:S(2)}) copy-start(bf16[4,4,16,512]{3,2,1,0:T(8,128)(2,1)} %get-tuple-element.34.refs_0_) | copy-start | bytes 786436
  13.8 17.5 %collective-permute-start.18 = (bf16[4,4,16,512]{3,2,1,0:T(8,128)(2,1)}, bf16[4,4,16,512]{3,2,1,0:T(8,128)(2,1)S(1)}, u32[]{:S(2)}, u32[]{:S(2)}) collective-permute-start(bf16[4,4,16,512]{3,2,1,0:T(8,128)(2,1)} %get-tuple-element.37), channel_id=1, source_target_pairs={{0,12},{1,13},{2,14},{3,15},{4,0},{5,1},{6,2},{7,3},{8,4},{9,5},{1... | collective-permute-start | bytes 786440 | tf_op jit(solution)/shard_map/ppermute | solution.py:255
  17.0 28.5 %collective-permute-start.4 = (bf16[2,2,320,256]{3,2,1,0:T(8,128)(2,1)S(1)}, bf16[2,2,320,256]{3,2,1,0:T(8,128)(2,1)S(1)}, u32[]{:S(2)}, u32[]{:S(2)}) collective-permute-start(bf16[2,2,320,256]{3,2,1,0:T(8,128)(2,1)S(1)} %get-tuple-element.25), channel_id=1, source_target_pairs={{0,16},{1,17},{2,18},{3,19},{4,20},{5,21},{6,22},{7,23},{8,24},{9,... | collective-permute-start | bytes 1966088 | tf_op jit(solution)/shard_map/ppermute | solution.py:255
  32.0 8.6 %collective-permute-start.21 = (bf16[4,4,16,512]{3,2,1,0:T(8,128)(2,1)S(1)}, bf16[4,4,16,512]{3,2,1,0:T(8,128)(2,1)S(1)}, u32[]{:S(2)}, u32[]{:S(2)}) collective-permute-start(bf16[4,4,16,512]{3,2,1,0:T(8,128)(2,1)S(1)} %get-tuple-element.41), channel_id=1, source_target_pairs={{0,3},{1,2},{2,1},{3,0},{4,7},{5,6},{6,5},{7,4},{8,11},{9,10},{10,... | collective-permute-start | bytes 786440 | tf_op jit(solution)/shard_map/ppermute | solution.py:255
  34.3 10.6 %collective-permute-start.10 = (bf16[2,1,320,256]{3,2,1,0:T(8,128)(2,1)S(1)}, bf16[2,1,320,256]{3,2,1,0:T(8,128)(2,1)S(1)}, u32[]{:S(2)}, u32[]{:S(2)}) collective-permute-start(bf16[2,1,320,256]{3,2,1,0:T(8,128)(2,1)S(1)} %get-tuple-element.31), channel_id=1, source_target_pairs={{0,16},{1,17},{2,18},{3,19},{4,20},{5,21},{6,22},{7,23},{8,24},{9,... | collective-permute-start | bytes 983048 | tf_op jit(solution)/shard_map/ppermute | solution.py:255
  35.9 13.3 %collective-permute-start.6 = (bf16[2,2,192,256]{3,2,1,0:T(8,128)(2,1)S(1)}, bf16[2,2,192,256]{3,2,1,0:T(8,128)(2,1)S(1)}, u32[]{:S(2)}, u32[]{:S(2)}) collective-permute-start(bf16[2,2,192,256]{3,2,1,0:T(8,128)(2,1)S(1)} %get-tuple-element.27), channel_id=1, source_target_pairs={{0,2},{1,3},{2,0},{3,1},{4,6},{5,7},{6,4},{7,5},{8,10},{9,11},{10,... | collective-permute-start | bytes 1179656 | tf_op jit(solution)/shard_map/ppermute | solution.py:255
  37.7 39.0 %collective-permute-start.2 = (bf16[2,1,512,256]{3,2,1,0:T(8,128)(2,1)S(1)}, bf16[2,1,512,256]{3,2,1,0:T(8,128)(2,1)S(1)}, u32[]{:S(2)}, u32[]{:S(2)}) collective-permute-start(bf16[2,1,512,256]{3,2,1,0:T(8,128)(2,1)S(1)} %get-tuple-element.23), channel_id=1, source_target_pairs={{0,16},{1,17},{2,18},{3,19},{4,20},{5,21},{6,22},{7,23},{8,24},{9,... | collective-permute-start | bytes 1572872 | tf_op jit(solution)/shard_map/ppermute | solution.py:255
  40.5 10.2 %collective-permute-start.20 = (bf16[4,4,16,512]{3,2,1,0:T(8,128)(2,1)S(1)}, bf16[4,4,16,512]{3,2,1,0:T(8,128)(2,1)S(1)}, u32[]{:S(2)}, u32[]{:S(2)}) collective-permute-start(bf16[4,4,16,512]{3,2,1,0:T(8,128)(2,1)S(1)} %get-tuple-element.40), channel_id=1, source_target_pairs={{0,1},{1,0},{2,3},{3,2},{4,5},{5,4},{6,7},{7,6},{8,9},{9,8},{10,11... | collective-permute-start | bytes 786440 | tf_op jit(solution)/shard_map/ppermute | solution.py:255
  45.0 8.4 %collective-permute-start.12 = (bf16[2,1,192,256]{3,2,1,0:T(8,128)(2,1)S(1)}, bf16[2,1,192,256]{3,2,1,0:T(8,128)(2,1)S(1)}, u32[]{:S(2)}, u32[]{:S(2)}) collective-permute-start(bf16[2,1,192,256]{3,2,1,0:T(8,128)(2,1)S(1)} %get-tuple-element.33), channel_id=1, source_target_pairs={{0,2},{1,3},{2,0},{3,1},{4,6},{5,7},{6,4},{7,5},{8,10},{9,11},{10,... | collective-permute-start | bytes 589832 | tf_op jit(solution)/shard_map/ppermute | solution.py:255
  45.5 13.5 %collective-permute-start.19 = (bf16[4,4,16,512]{3,2,1,0:T(8,128)(2,1)S(1)}, bf16[4,4,16,512]{3,2,1,0:T(8,128)(2,1)S(1)}, u32[]{:S(2)}, u32[]{:S(2)}) collective-permute-start(bf16[4,4,16,512]{3,2,1,0:T(8,128)(2,1)S(1)} %get-tuple-element.39), channel_id=1, source_target_pairs={{0,2},{1,3},{2,0},{3,1},{4,6},{5,7},{6,4},{7,5},{8,10},{9,11},{10,... | collective-permute-start | bytes 786440 | tf_op jit(solution)/shard_map/ppermute | solution.py:255
  49.2 27.9 %collective-permute-start.5 = (bf16[2,320,256]{2,1,0:T(8,128)(2,1)S(1)}, bf16[2,320,256]{2,1,0:T(8,128)(2,1)S(1)}, u32[]{:S(2)}, u32[]{:S(2)}) collective-permute-start(bf16[2,320,256]{2,1,0:T(8,128)(2,1)S(1)} %shard_map.81), channel_id=1, source_target_pairs={{0,2},{1,3},{2,0},{3,1},{4,6},{5,7},{6,4},{7,5},{8,10},{9,11},{10,... | collective-permute-start | bytes 983048 | tf_op jit(solution)/shard_map/ppermute | solution.py:255
  50.8 18.6 %collective-permute-start.11 = (bf16[1,320,256]{2,1,0:T(8,128)(2,1)S(1)}, bf16[1,320,256]{2,1,0:T(8,128)(2,1)S(1)}, u32[]{:S(2)}, u32[]{:S(2)}) collective-permute-start(bf16[1,320,256]{2,1,0:T(8,128)(2,1)S(1)} %shard_map.85), channel_id=1, source_target_pairs={{0,2},{1,3},{2,0},{3,1},{4,6},{5,7},{6,4},{7,5},{8,10},{9,11},{10,... | collective-permute-start | bytes 491528 | tf_op jit(solution)/shard_map/ppermute | solution.py:255
  53.4 23.7 %collective-permute-start.7 = (bf16[2,192,256]{2,1,0:T(8,128)(2,1)S(1)}, bf16[2,192,256]{2,1,0:T(8,128)(2,1)S(1)}, u32[]{:S(2)}, u32[]{:S(2)}) collective-permute-start(bf16[2,192,256]{2,1,0:T(8,128)(2,1)S(1)} %shard_map.82), channel_id=1, source_target_pairs={{0,16},{1,17},{2,18},{3,19},{4,20},{5,21},{6,22},{7,23},{8,24},{9,... | collective-permute-start | bytes 589832 | tf_op jit(solution)/shard_map/ppermute | solution.py:255
  59.0 4.6 %collective-permute-start.13 = (bf16[1,192,256]{2,1,0:T(8,128)(2,1)S(1)}, bf16[1,192,256]{2,1,0:T(8,128)(2,1)S(1)}, u32[]{:S(2)}, u32[]{:S(2)}) collective-permute-start(bf16[1,192,256]{2,1,0:T(8,128)(2,1)S(1)} %shard_map.86), channel_id=1, source_target_pairs={{0,16},{1,17},{2,18},{3,19},{4,20},{5,21},{6,22},{7,23},{8,24},{9,... | collective-permute-start | bytes 294920 | tf_op jit(solution)/shard_map/ppermute | solution.py:255
  69.5 15.4 %collective-permute-start.14 = (bf16[512,256]{1,0:T(8,128)(2,1)S(1)}, bf16[512,256]{1,0:T(8,128)(2,1)S(1)}, u32[]{:S(2)}, u32[]{:S(2)}) collective-permute-start(bf16[512,256]{1,0:T(8,128)(2,1)S(1)} %shard_map.87), channel_id=1, source_target_pairs={{0,12},{1,13},{2,14},{3,15},{4,0},{5,1},{6,2},{7,3},{8,4},{9,5},{1... | collective-permute-start | bytes 786440 | tf_op jit(solution)/shard_map/ppermute | solution.py:255
  76.7 2.3 %copy-start.3 = (s32[32]{0:T(128)S(1)}, s32[32]{0:T(128)}, u32[]{:S(2)}) copy-start(s32[32]{0:T(128)} %param.11) | copy-start | bytes 388
  76.7 8.0 %collective-permute-start.3 = (bf16[1,512,256]{2,1,0:T(8,128)(2,1)S(1)}, bf16[1,512,256]{2,1,0:T(8,128)(2,1)S(1)}, u32[]{:S(2)}, u32[]{:S(2)}) collective-permute-start(bf16[1,512,256]{2,1,0:T(8,128)(2,1)S(1)} %shard_map.78), channel_id=1, source_target_pairs={{0,2},{1,3},{2,0},{3,1},{4,6},{5,7},{6,4},{7,5},{8,10},{9,11},{10,... | collective-permute-start | bytes 786440 | tf_op jit(solution)/shard_map/ppermute | solution.py:255
  77.3 22.8 %collective-permute-start.9 = (bf16[512,256]{1,0:T(8,128)(2,1)S(1)}, bf16[512,256]{1,0:T(8,128)(2,1)S(1)}, u32[]{:S(2)}, u32[]{:S(2)}) collective-permute-start(bf16[512,256]{1,0:T(8,128)(2,1)S(1)} %get-tuple-element.29), channel_id=1, source_target_pairs={{0,8},{1,9},{2,10},{3,11},{4,12},{5,13},{6,14},{7,15},{8,0},{9,1},... | collective-permute-start | bytes 786440 | tf_op jit(solution)/shard_map/ppermute | solution.py:255
  79.0 21.1 %collective-permute-start.8 = (bf16[512,256]{1,0:T(8,128)(2,1)S(1)}, bf16[512,256]{1,0:T(8,128)(2,1)S(1)}, u32[]{:S(2)}, u32[]{:S(2)}) collective-permute-start(bf16[512,256]{1,0:T(8,128)(2,1)S(1)} %get-tuple-element.28), channel_id=1, source_target_pairs={{0,4},{1,5},{2,6},{3,7},{4,8},{5,9},{6,10},{7,11},{8,12},{9,13},{1... | collective-permute-start | bytes 786440 | tf_op jit(solution)/shard_map/ppermute | solution.py:255
  79.8 22.0 %collective-permute-start.22 = (bf16[16,32,512]{2,1,0:T(8,128)(2,1)S(1)}, bf16[16,32,512]{2,1,0:T(8,128)(2,1)S(1)}, u32[]{:S(2)}, u32[]{:S(2)}) collective-permute-start(bf16[16,32,512]{2,1,0:T(8,128)(2,1)S(1)} %fusion), channel_id=1, source_target_pairs={{0,16},{1,17},{2,18},{3,19},{4,20},{5,21},{6,22},{7,23},{8,24},{9,... | collective-permute-start | bytes 1572872 | tf_op jit(solution)/shard_map/ppermute | solution.py:255
  100.2 7.3 %collective-permute-start.15 = (bf16[512,256]{1,0:T(8,128)(2,1)S(1)}, bf16[512,256]{1,0:T(8,128)(2,1)S(1)}, u32[]{:S(2)}, u32[]{:S(2)}) collective-permute-start(bf16[512,256]{1,0:T(8,128)(2,1)S(1)} %get-tuple-element.44), channel_id=1, source_target_pairs={{0,16},{1,17},{2,18},{3,19},{4,20},{5,21},{6,22},{7,23},{8,24},{9,... | collective-permute-start | bytes 786440 | tf_op jit(solution)/shard_map/ppermute | solution.py:255
